TPU v7x, 64 devices: a 2x2x8 block of a 4x4x8 slice. The times are simulated.
64 devices in a mesh: rep: 8 (over x, y, core), dp: 8 (over z).
Axes of the slice: x: 2, y: 2, z: 8, core: 2. Of those that a mesh axis runs over, the one named last changes fastest.
The devices are a block of a 4x4x8 slice.
Arguments:
- x: bfloat16 [64, 2048, 640], P(('rep', 'dp')), parts along dimension 0
- dy: bfloat16 [64, 2048, 640], P(('rep', 'dp')), parts along dimension 0
- w_gate: bfloat16 [2, 640, 1536], P(None, 'dp')
- w_up: bfloat16 [2, 640, 1536], P(None, 'dp')
- w_down: bfloat16 [2, 1536, 640], P(None, 'dp')
- m_w_gate: float32 [2, 640, 1536], P(None, 'dp')
- m_w_up: float32 [2, 640, 1536], P(None, 'dp')
- m_w_down: float32 [2, 1536, 640], P(None, 'dp')
- v_w_gate: float32 [2, 640, 1536], P(None, 'dp')
- v_w_up: float32 [2, 640, 1536], P(None, 'dp')
- v_w_down: float32 [2, 1536, 640], P(None, 'dp')
Outputs:
- output 1: bfloat16 [16, 640, 1536], P('rep', 'dp'), parts along dimension 0
- output 2: bfloat16 [16, 640, 1536], P('rep', 'dp'), parts along dimension 0
- output 3: bfloat16 [16, 1536, 640], P('rep', 'dp'), parts along dimension 0
- output 4: float32 [16, 640, 1536], P('rep', 'dp'), parts along dimension 0
- output 5: float32 [16, 640, 1536], P('rep', 'dp'), parts along dimension 0
- output 6: float32 [16, 1536, 640], P('rep', 'dp'), parts along dimension 0
- output 7: float32 [16, 640, 1536], P('rep', 'dp'), parts along dimension 0
- output 8: float32 [16, 640, 1536], P('rep', 'dp'), parts along dimension 0
- output 9: float32 [16, 1536, 640], P('rep', 'dp'), parts along dimension 0
There are 8 independent parts. A program takes and returns all parts, laid end to end along the dimension named above; an argument that names none is the same for every part.
All inputs are finite; a program needn't handle non-finite values.
Results may differ from a plain program's by a relative error of at most 0.022.
Values are sent between devices in bfloat16 or wider.
A program may use at most 768 MiB of HBM per device.

v0:
```python
import jax
import jax.numpy as jnp
from jax import lax
from jax.sharding import PartitionSpec as P

NAMES = ("w_gate", "w_up", "w_down")


def matmul(a, w):
    return jnp.dot(a, w, preferred_element_type=jnp.float32).astype(jnp.bfloat16)


def normed(h):
    wide = h.astype(jnp.float32)
    scale = lax.rsqrt(jnp.mean(wide**2, -1, keepdims=True) + 1e-6)
    return (wide * scale).astype(jnp.bfloat16)


def layer(h, w):
    a = normed(h)
    gate = jnp.dot(a, w["w_gate"], preferred_element_type=jnp.float32)
    up = jnp.dot(a, w["w_up"], preferred_element_type=jnp.float32)
    return h + matmul((jax.nn.silu(gate) * up).astype(jnp.bfloat16), w["w_down"])


def adamw(w, m, v, g):
    m = 0.9 * m + 0.1 * g
    v = 0.95 * v + 0.05 * g * g
    step = m * lax.rsqrt(v + 1e-8) + 0.1 * w
    return (w - 0.02 * step).astype(jnp.bfloat16), m, v


def clipped(gradients, sum_of_squares, count):
    factor = jnp.minimum(1.0, 0.5 * lax.rsqrt(sum_of_squares / count + 1e-30))
    return [g * factor for g in gradients]


def solution(mesh):
    def fetched(weights, number):
        return {name: lax.all_gather(w[number], "dp", axis=0, tiled=True) for name, w in zip(NAMES, weights, strict=True)}

    def step(x, dy, *arrays):
        weights, m, v = (arrays[i : i + 3] for i in (0, 3, 6))
        layers = weights[0].shape[0]
        h, kept = x[0], []
        for number in range(layers):
            kept.append(h)
            h = layer(h, fetched(weights, number))
        by_h, mine = dy[0], [None] * layers
        for number in reversed(range(layers)):
            _, back = jax.vjp(lambda w, h: layer(h, w), fetched(weights, number), kept[number])
            by_w, by_h = back(by_h)
            mine[number] = [lax.psum_scatter(by_w[name], "dp", scatter_dimension=0, tiled=True) for name in NAMES]
        gradients = [jnp.stack([mine[number][i] for number in range(layers)]).astype(jnp.float32) for i in range(3)]
        squares = lax.psum(sum(jnp.sum(g * g) for g in gradients), "dp")
        gradients = clipped(gradients, squares, lax.psum(1, "dp") * sum(g.size for g in gradients))
        new = [adamw(w.astype(jnp.float32), m, v, g) for w, m, v, g in zip(weights, m, v, gradients, strict=True)]
        return tuple(one[which] for which in range(3) for one in new)

    states, cut = P(("rep", "dp"), None, None), P(None, "dp", None)
    return jax.shard_map(
        step,
        mesh=mesh,
        in_specs=(states, states) + (cut,) * 9,
        out_specs=(P("rep", "dp", None),) * 9,
        check_vma=False,
    )
```

profile of v0, /device:TPU:22, one launch (start us, length us, event | category | flops | bytes accessed | tf_op | source)
XLA Modules:
  0.0 555.4 jit_solution(4696487027399735490)
XLA Ops:
  7.2 0.1 all-gather.13.cloned.1.call-start
  7.3 1.9 fusion.90
  9.1 0.1 all-gather.13.cloned.1.call-update
  9.2 0.1 all-gather.15.cloned.1.call-start
  9.3 1.9 fusion.89
  11.1 0.1 all-gather.15.cloned.1.call-update
  11.2 0.1 all-gather.17.cloned.1.call-start
  11.3 1.9 fusion.88
  13.1 0.1 all-gather.17.cloned.1.call-update
  13.2 0.1 all-gather.21.cloned.1.call-start
  13.3 0.6 all-gather.21.cloned.1.call-update
  13.9 0.1 all-gather.23.cloned.1.call-start
  13.9 0.6 all-gather.23.cloned.1.call-update
  14.5 0.1 all-gather.19.cloned.1.call-start
  14.6 0.6 all-gather.19.cloned.1.call-update
  15.1 0.1 reduce-scatter.15.cloned.1.call-start
  15.2 3.0 copy.20
  18.2 0.6 fusion.15
  18.8 4.5 copy.21
  23.3 27.7 %all-gather.13.cloned.1.call-done = bf16[1,640,1536]{2,1,0:T(8,128)(2,1)} async-done(((bf16[1,80,1536]{2,1,0:T(8,128)(2,1)}), bf16[1,640,1536]{2,1,0:T(8,128)(2,1)}) %all-gather.13.cloned.1.call-update) | async-done | bytes 1966096 | tf_op jit(solution)/shard_map/all_gather | solution.py:40
  51.0 9.5 %fusion.45 = f32[2048,1536]{1,0:T(8,128)} fusion(bf16[1,640,1536]{2,1,0:T(8,128)(2,1)} %all-gather.13.cloned.1.call-done, bf16[1,2048,640]{1,2,0:T(8,128)(2,1)S(1)} %copy.20, f32[2048]{0:T(1024)S(1)} %add_rsqrt_fusion), kind=kOutput, calls=%fused_computation.65 | convolution fusion | flops 4030464000 | bytes 17178624 | tf_op jit(solution)/shard_map/dot_general | solution.py:21
  60.4 28.3 %all-gather.15.cloned.1.call-done = bf16[1,640,1536]{2,1,0:T(8,128)(2,1)} async-done(((bf16[1,80,1536]{2,1,0:T(8,128)(2,1)}), bf16[1,640,1536]{2,1,0:T(8,128)(2,1)}) %all-gather.15.cloned.1.call-update) | async-done | bytes 1966096 | tf_op jit(solution)/shard_map/all_gather | solution.py:40
  88.8 13.9 %multiply_convert_fusion.1 = (bf16[2048,1536]{1,0:T(8,128)(2,1)}, f32[2048,1536]{1,0:T(8,128)}) fusion(f32[2048,1536]{1,0:T(8,128)} %fusion.45, bf16[1,640,1536]{2,1,0:T(8,128)(2,1)} %all-gather.15.cloned.1.call-done, bf16[1,2048,640]{1,2,0:T(8,128)(2,1)S(1)} %copy.20, f32[2048]{0:T(1024)S(1)} %add_rsqrt_fusion), kind=kOutput, calls=%fused_computation.17 | convolution fusion | flops 4049338368 | bytes 36052992 | tf_op jit(solution)/shard_map/dot_general | solution.py:22
  102.7 23.9 %all-gather.17.cloned.1.call-done = bf16[1,1536,640]{2,1,0:T(8,128)(2,1)} async-done(((bf16[1,192,640]{2,1,0:T(8,128)(2,1)}), bf16[1,1536,640]{2,1,0:T(8,128)(2,1)}) %all-gather.17.cloned.1.call-update) | async-done | bytes 1966096 | tf_op jit(solution)/shard_map/all_gather | solution.py:40
  126.6 9.6 %fusion.19 = (f32[2048]{0:T(1024)S(1)}, bf16[2048,640]{0,1:T(8,128)(2,1)}) fusion(bf16[2048,1536]{1,0:T(8,128)(2,1)} %get-tuple-element.24, bf16[1,1536,640]{2,1,0:T(8,128)(2,1)} %all-gather.17.cloned.1.call-done, bf16[1,2048,640]{1,2,0:T(8,128)(2,1)S(1)} %copy.20), kind=kOutput, calls=%fused_computation.37 | convolution fusion | flops 4033083392 | bytes 13508608 | tf_op jit(solution)/shard_map/dot_general | solution.py:10
  136.1 28.1 %all-gather.21.cloned.1.call-done = bf16[1,1536,640]{2,1,0:T(8,128)(2,1)} async-done(((bf16[1,192,640]{2,1,0:T(8,128)(2,1)}), bf16[1,1536,640]{2,1,0:T(8,128)(2,1)}) %all-gather.21.cloned.1.call-update) | async-done | bytes 1966096 | tf_op jit(solution)/shard_map/all_gather | solution.py:40
  164.2 9.6 %convolution_convert_fusion.1 = bf16[2048,1536]{1,0:T(8,128)(2,1)} fusion(bf16[1,2048,640]{2,1,0:T(8,128)(2,1)} %param.12, bf16[1,1536,640]{2,1,0:T(8,128)(2,1)} %all-gather.21.cloned.1.call-done), kind=kOutput, calls=%fused_computation.27 | convolution fusion | flops 4029677568 | bytes 10878976 | tf_op jit(solution)/shard_map/transpose(jvp())/dot_general | solution.py:10
  173.8 28.0 %all-gather.23.cloned.1.call-done = bf16[1,640,1536]{2,1,0:T(8,128)(2,1)} async-done(((bf16[1,80,1536]{2,1,0:T(8,128)(2,1)}), bf16[1,640,1536]{2,1,0:T(8,128)(2,1)}) %all-gather.23.cloned.1.call-update) | async-done | bytes 1966096 | tf_op jit(solution)/shard_map/all_gather | solution.py:40
  201.8 9.9 %fusion.34 = f32[2048,1536]{1,0:T(8,128)} fusion(bf16[1,640,1536]{2,1,0:T(8,128)(2,1)} %all-gather.23.cloned.1.call-done, bf16[2048,640]{0,1:T(8,128)(2,1)} %get-tuple-element.27, f32[2048]{0:T(1024)S(1)} %fusion.76), kind=kOutput, calls=%fused_computation.54 | convolution fusion | flops 4030464000 | bytes 17178624 | tf_op jit(solution)/shard_map/jvp()/dot_general | solution.py:22
  211.7 27.8 %all-gather.19.cloned.1.call-done = bf16[1,640,1536]{2,1,0:T(8,128)(2,1)} async-done(((bf16[1,80,1536]{2,1,0:T(8,128)(2,1)}), bf16[1,640,1536]{2,1,0:T(8,128)(2,1)}) %all-gather.19.cloned.1.call-update) | async-done | bytes 1966096 | tf_op jit(solution)/shard_map/all_gather | solution.py:40
  239.5 19.5 %fusion.2 = (bf16[2048,1536]{1,0:T(8,128)(2,1)}, f32[2048,1536]{1,0:T(8,128)}) fusion(f32[2048,1536]{1,0:T(8,128)} %fusion.34, bf16[2048,1536]{1,0:T(8,128)(2,1)} %convolution_convert_fusion.1, bf16[1,640,1536]{2,1,0:T(8,128)(2,1)} %all-gather.19.cloned.1.call-done, bf16[2048,640]{0,1:T(8,128)(2,1)} %get-tuple-element.27, f32[2048]{0:T(1024)S(1)} %fusion.76), kind=kOutput, calls=%fused_computation.8 | convolution fusion | flops 4068212736 | bytes 42344448 | tf_op jit(solution)/shard_map/jvp()/dot_general | solution.py:21
  259.0 7.6 %fusion.23 = bf16[2048,640]{0,1:T(8,128)(2,1)S(1)} fusion(bf16[2048,1536]{1,0:T(8,128)(2,1)S(1)} %copy-done.20, bf16[1,640,1536]{2,1,0:T(8,128)(2,1)S(1)} %copy-done.17, f32[2048,1536]{1,0:T(8,128)} %get-tuple-element.29), kind=kOutput, calls=%fused_computation.41 | convolution fusion | flops 4046716928 | bytes 23461888 | tf_op jit(solution)/shard_map/transpose(jvp())/dot_general | solution.py:22
  266.6 7.9 %fusion.21 = (f32[2048]{0:T(1024)S(1)}, bf16[2048,640]{0,1:T(8,128)(2,1)S(1)}) fusion(bf16[2048,640]{0,1:T(8,128)(2,1)S(1)} %copy-done.1, bf16[2048,640]{0,1:T(8,128)(2,1)S(1)} %fusion.23, bf16[2048,1536]{1,0:T(8,128)(2,1)} %get-tuple-element.28, bf16[1,640,1536]{2,1,0:T(8,128)(2,1)S(1)} %copy-done.18), kind=kOutput, calls=%fused_computation.39 | convolution fusion | flops 4033083392 | bytes 16130048 | tf_op jit(solution)/shard_map/transpose(jvp())/dot_general | solution.py:21
  274.5 1.8 fusion.29
  276.3 1.5 copy-done.2
  277.8 8.1 %convolution_convert_fusion.2 = bf16[1536,640]{1,0:T(8,128)(2,1)} fusion(bf16[2048,1536]{1,0:T(8,128)(2,1)} %get-tuple-element.24, bf16[2048,640]{0,1:T(8,128)(2,1)S(1)} %fusion.29), kind=kOutput, calls=%fused_computation.45 | convolution fusion | flops 4027514880 | bytes 10878976 | tf_op jit(solution)/shard_map/transpose(jvp())/dot_general | solution.py:10
  285.9 0.1 reduce-scatter.15.cloned.1.call-update
  286.0 0.1 reduce-scatter.17.cloned.1.call-start
  286.1 12.8 %fusion.22 = bf16[1536,640]{1,0:T(8,128)(2,1)} fusion(f32[2048,1536]{1,0:T(8,128)} %fusion.34, bf16[1,2048,640]{2,1,0:T(8,128)(2,1)} %param.12, f32[2048,1536]{1,0:T(8,128)} %get-tuple-element.29), kind=kOutput, calls=%fused_computation.40 | convolution fusion | flops 4046389248 | bytes 29753344 | tf_op jit(solution)/shard_map/transpose(jvp())/dot_general | solution.py:10
  298.9 0.1 reduce-scatter.17.cloned.1.call-update
  299.0 0.1 reduce-scatter.11.cloned.1.call-start
  299.0 7.7 %convolution_convert_fusion = bf16[2048,1536]{1,0:T(8,128)(2,1)S(1)} fusion(bf16[2048,640]{0,1:T(8,128)(2,1)} %copy-done.2, bf16[1,1536,640]{2,1,0:T(8,128)(2,1)} %all-gather.17.cloned.1.call-done), kind=kOutput, calls=%fused_computation.26 | convolution fusion | flops 4029677568 | bytes 10878976 | tf_op jit(solution)/shard_map/transpose(jvp())/dot_general | solution.py:10
  306.7 2.6 copy-done.19
  309.3 9.2 %fusion.28 = bf16[640,1536]{1,0:T(8,128)(2,1)} fusion(bf16[2048,1536]{1,0:T(8,128)(2,1)S(1)} %convolution_convert_fusion, f32[2048,1536]{1,0:T(8,128)} %fusion.45, bf16[1,2048,640]{1,2,0:T(8,128)(2,1)S(1)} %copy.20, f32[2048]{0:T(1024)S(1)} %copy-done.16), kind=kOutput, calls=%fused_computation.44 | convolution fusion | flops 4050321408 | bytes 23470080 | tf_op jit(solution)/shard_map/transpose(jvp())/dot_general | solution.py:22
  318.5 0.1 reduce-scatter.11.cloned.1.call-update
  318.6 0.1 reduce-scatter.13.cloned.1.call-start
  318.6 10.8 %fusion.24 = bf16[640,1536]{1,0:T(8,128)(2,1)} fusion(bf16[2048,1536]{1,0:T(8,128)(2,1)} %convolution_convert_fusion.1, bf16[2048,640]{0,1:T(8,128)(2,1)} %get-tuple-element.27, f32[2048]{0:T(1024)S(1)} %fusion.76, f32[2048,1536]{1,0:T(8,128)} %get-tuple-element.29), kind=kOutput, calls=%fused_computation.42 | convolution fusion | flops 4050321408 | bytes 23470080 | tf_op jit(solution)/shard_map/transpose(jvp())/dot_general | solution.py:22
  329.5 0.1 reduce-scatter.13.cloned.1.call-update
  329.5 0.1 reduce-scatter.7.cloned.1.call-start
  329.6 14.6 %fusion.25 = bf16[640,1536]{1,0:T(8,128)(2,1)} fusion(f32[2048,1536]{1,0:T(8,128)} %fusion.45, f32[2048,1536]{1,0:T(8,128)} %get-tuple-element.25, bf16[2048,1536]{1,0:T(8,128)(2,1)} %copy-done.19, bf16[1,2048,640]{1,2,0:T(8,128)(2,1)S(1)} %copy.20, f32[2048]{0:T(1024)S(1)} %copy-done.16), kind=kOutput, calls=%fused_computation.43 | convolution fusion | flops 4066050048 | bytes 36052992 | tf_op jit(solution)/shard_map/transpose(jvp())/dot_general | solution.py:21
  344.2 0.1 reduce-scatter.7.cloned.1.call-update
  344.3 0.3 reduce-scatter.9.cloned.1.call-start
  344.6 9.2 %convolution_convert_fusion.3 = bf16[640,1536]{1,0:T(8,128)(2,1)} fusion(bf16[2048,1536]{1,0:T(8,128)(2,1)} %get-tuple-element.28, bf16[2048,640]{0,1:T(8,128)(2,1)} %get-tuple-element.27, f32[2048]{0:T(1024)S(1)} %fusion.76), kind=kOutput, calls=%fused_computation.46 | convolution fusion | flops 4030464000 | bytes 10887168 | tf_op jit(solution)/shard_map/transpose(jvp())/dot_general | solution.py:21
  353.9 9.0 %reduce-scatter.17.cloned.1.call-done = bf16[192,640]{1,0:T(8,128)(2,1)} async-done(((bf16[1536,640]{1,0:T(8,128)(2,1)}), bf16[192,640]{1,0:T(8,128)(2,1)}) %reduce-scatter.17.cloned.1.call-update) | async-done | bytes 245776 | tf_op jit(solution)/shard_map/reduce_scatter | solution.py:53
  362.9 1.9 fusion.66
  364.8 37.7 %reduce-scatter.11.cloned.1.call-done = bf16[80,1536]{1,0:T(8,128)(2,1)} async-done(((bf16[640,1536]{1,0:T(8,128)(2,1)}), bf16[80,1536]{1,0:T(8,128)(2,1)}) %reduce-scatter.11.cloned.1.call-update) | async-done | bytes 245776 | tf_op jit(solution)/shard_map/reduce_scatter | solution.py:53
  402.6 39.5 %reduce-scatter.13.cloned.1.call-done = bf16[80,1536]{1,0:T(8,128)(2,1)} async-done(((bf16[640,1536]{1,0:T(8,128)(2,1)}), bf16[80,1536]{1,0:T(8,128)(2,1)}) %reduce-scatter.13.cloned.1.call-update) | async-done | bytes 245776 | tf_op jit(solution)/shard_map/reduce_scatter | solution.py:53
  442.0 2.0 fusion.65
  444.0 37.6 %reduce-scatter.7.cloned.1.call-done = bf16[80,1536]{1,0:T(8,128)(2,1)} async-done(((bf16[640,1536]{1,0:T(8,128)(2,1)}), bf16[80,1536]{1,0:T(8,128)(2,1)}) %reduce-scatter.7.cloned.1.call-update) | async-done | bytes 245776 | tf_op jit(solution)/shard_map/reduce_scatter | solution.py:53
  481.6 39.5 %reduce-scatter.9.cloned.1.call-done = bf16[80,1536]{1,0:T(8,128)(2,1)} async-done(((bf16[640,1536]{1,0:T(8,128)(2,1)}), bf16[80,1536]{1,0:T(8,128)(2,1)}) %reduce-scatter.9.cloned.1.call-update) | async-done | bytes 245776 | tf_op jit(solution)/shard_map/reduce_scatter | solution.py:53
  521.1 2.0 fusion.64
  525.0 16.1 %psum.7 = f32[]{:T(128)} all-reduce(f32[]{:T(128)S(6)} %add.99), channel_id=1, replica_groups=mesh['rep'=8,'dp'=8] {'dp'}, use_global_device_ids=true, to_apply=%region_12.13 | all-reduce | flops 1 | bytes 8 | tf_op jit(solution)/shard_map/psum | solution.py:55
  541.8 3.3 fusion.72
  545.2 2.9 fusion.63
  (45 shorter events, 0.2 us)
Async XLA Ops:
  7.2 43.8 %all-gather.13.cloned.1.call-start = ((), (), s32[]{:S(2)}) async-start(), calls=%async_computation.12 | async-start | bytes 2211840 | tf_op jit(solution)/shard_map/all_gather | solution.py:40
  9.2 79.6 %all-gather.15.cloned.1.call-start = ((), (), s32[]{:S(2)}) async-start(), calls=%async_computation.13 | async-start | bytes 2211840 | tf_op jit(solution)/shard_map/all_gather | solution.py:40
  11.2 115.4 %all-gather.17.cloned.1.call-start = ((), (), s32[]{:S(2)}) async-start(), calls=%async_computation.14 | async-start | bytes 2211840 | tf_op jit(solution)/shard_map/all_gather | solution.py:40
  13.2 151.0 %all-gather.21.cloned.1.call-start = ((), (), s32[]{:S(2)}) async-start(), calls=%async_computation.16 | async-start | bytes 2211840 | tf_op jit(solution)/shard_map/all_gather | solution.py:40
  13.9 188.0 %all-gather.23.cloned.1.call-start = ((), (), s32[]{:S(2)}) async-start(), calls=%async_computation.17 | async-start | bytes 2211840 | tf_op jit(solution)/shard_map/all_gather | solution.py:40
  14.5 225.0 %all-gather.19.cloned.1.call-start = ((), (), s32[]{:S(2)}) async-start(), calls=%async_computation.15 | async-start | bytes 2211840 | tf_op jit(solution)/shard_map/all_gather | solution.py:40
  15.1 338.8 %reduce-scatter.15.cloned.1.call-start = ((), (), s32[]{:S(2)}) async-start(), calls=%async_computation.10 | async-start | bytes 2211840 | tf_op jit(solution)/shard_map/reduce_scatter | solution.py:53
  18.8 70.0 %copy-start.15 = (f32[2048]{0:T(1024)}, f32[2048]{0:T(1024)S(1)}, u32[]{:S(2)}) copy-start(f32[2048]{0:T(1024)S(1)} %add_rsqrt_fusion) | copy-start | bytes 24580
  239.5 19.5 %copy-start.17 = (bf16[1,640,1536]{2,1,0:T(8,128)(2,1)S(1)}, bf16[1,640,1536]{2,1,0:T(8,128)(2,1)}, u32[]{:S(2)}) copy-start(bf16[1,640,1536]{2,1,0:T(8,128)(2,1)} %all-gather.23.cloned.1.call-done) | copy-start | bytes 5898244
  239.5 19.5 %copy-start.20 = (bf16[2048,1536]{1,0:T(8,128)(2,1)S(1)}, bf16[2048,1536]{1,0:T(8,128)(2,1)}, u32[]{:S(2)}) copy-start(bf16[2048,1536]{1,0:T(8,128)(2,1)} %convolution_convert_fusion.1) | copy-start | bytes 18874372
  258.9 7.7 %copy-start.1 = (bf16[2048,640]{0,1:T(8,128)(2,1)S(1)}, bf16[2048,640]{0,1:T(8,128)(2,1)}, u32[]{:S(2)}) copy-start(bf16[2048,640]{0,1:T(8,128)(2,1)} %get-tuple-element.27) | copy-start | bytes 7864324
  259.0 7.7 %copy-start.18 = (bf16[1,640,1536]{2,1,0:T(8,128)(2,1)S(1)}, bf16[1,640,1536]{2,1,0:T(8,128)(2,1)}, u32[]{:S(2)}) copy-start(bf16[1,640,1536]{2,1,0:T(8,128)(2,1)} %all-gather.19.cloned.1.call-done) | copy-start | bytes 5898244
  266.6 7.9 %copy-start = (bf16[1,2048,640]{1,2,0:T(8,128)(2,1)S(1)}, bf16[1,2048,640]{1,2,0:T(8,128)(2,1)}, u32[]{:S(2)}) copy-start(bf16[1,2048,640]{1,2,0:T(8,128)(2,1)} %copy.21) | copy-start | bytes 7864324
  276.3 1.5 copy-start.2
  286.0 76.9 %reduce-scatter.17.cloned.1.call-start = ((), (), s32[]{:S(2)}) async-start(), calls=%async_computation.11 | async-start | bytes 2211840 | tf_op jit(solution)/shard_map/reduce_scatter | solution.py:53
  299.0 10.4 %copy-start.16 = (f32[2048]{0:T(1024)S(1)}, f32[2048]{0:T(1024)}, u32[]{:S(2)}) copy-start(f32[2048]{0:T(1024)} %copy-done.15) | copy-start | bytes 24580
  299.0 103.6 %reduce-scatter.11.cloned.1.call-start = ((), (), s32[]{:S(2)}) async-start(), calls=%async_computation.8 | async-start | bytes 2211840 | tf_op jit(solution)/shard_map/reduce_scatter | solution.py:53
  306.7 2.6 copy-start.19
  318.6 123.4 %reduce-scatter.13.cloned.1.call-start = ((), (), s32[]{:S(2)}) async-start(), calls=%async_computation.9 | async-start | bytes 2211840 | tf_op jit(solution)/shard_map/reduce_scatter | solution.py:53
  329.5 152.1 %reduce-scatter.7.cloned.1.call-start = ((), (), s32[]{:S(2)}) async-start(), calls=%async_computation.6 | async-start | bytes 2211840 | tf_op jit(solution)/shard_map/reduce_scatter | solution.py:53
  344.3 197.5 %copy-start.5 = (bf16[2,192,640]{2,1,0:T(8,128)(2,1)S(1)}, bf16[2,192,640]{2,1,0:T(8,128)(2,1)}, u32[]{:S(2)}) copy-start(bf16[2,192,640]{2,1,0:T(8,128)(2,1)} %param.15) | copy-start | bytes 1474564
  344.3 197.5 %copy-start.10 = (f32[2,192,640]{2,1,0:T(8,128)S(1)}, f32[2,192,640]{2,1,0:T(8,128)}, u32[]{:S(2)}) copy-start(f32[2,192,640]{2,1,0:T(8,128)} %param.21) | copy-start | bytes 2949124
  344.3 176.8 %reduce-scatter.9.cloned.1.call-start = ((), (), s32[]{:S(2)}) async-start(), calls=%async_computation.7 | async-start | bytes 2211840 | tf_op jit(solution)/shard_map/reduce_scatter | solution.py:53
  353.8 191.3 %copy-start.3 = (bf16[2,80,1536]{2,1,0:T(8,128)(2,1)S(1)}, bf16[2,80,1536]{2,1,0:T(8,128)(2,1)}, u32[]{:S(2)}) copy-start(bf16[2,80,1536]{2,1,0:T(8,128)(2,1)} %param.13) | copy-start | bytes 1474564
  353.8 191.3 %copy-start.4 = (bf16[2,80,1536]{2,1,0:T(8,128)(2,1)S(1)}, bf16[2,80,1536]{2,1,0:T(8,128)(2,1)}, u32[]{:S(2)}) copy-start(bf16[2,80,1536]{2,1,0:T(8,128)(2,1)} %param.14) | copy-start | bytes 1474564
  402.6 142.6 %copy-start.6 = (bf16[80,1536]{1,0:T(8,128)(2,1)S(1)}, bf16[80,1536]{1,0:T(8,128)(2,1)}, u32[]{:S(2)}) copy-start(bf16[80,1536]{1,0:T(8,128)(2,1)} %reduce-scatter.11.cloned.1.call-done) | copy-start | bytes 737284
  442.0 103.1 %copy-start.7 = (bf16[80,1536]{1,0:T(8,128)(2,1)S(1)}, bf16[80,1536]{1,0:T(8,128)(2,1)}, u32[]{:S(2)}) copy-start(bf16[80,1536]{1,0:T(8,128)(2,1)} %reduce-scatter.13.cloned.1.call-done) | copy-start | bytes 737284
  481.6 63.5 %copy-start.8 = (bf16[80,1536]{1,0:T(8,128)(2,1)S(1)}, bf16[80,1536]{1,0:T(8,128)(2,1)}, u32[]{:S(2)}) copy-start(bf16[80,1536]{1,0:T(8,128)(2,1)} %reduce-scatter.7.cloned.1.call-done) | copy-start | bytes 737284
  521.1 24.0 %copy-start.9 = (bf16[80,1536]{1,0:T(8,128)(2,1)S(1)}, bf16[80,1536]{1,0:T(8,128)(2,1)}, u32[]{:S(2)}) copy-start(bf16[80,1536]{1,0:T(8,128)(2,1)} %reduce-scatter.9.cloned.1.call-done) | copy-start | bytes 737284
  541.8 3.4 copy-start.11
  541.8 3.4 copy-start.12
  541.8 3.4 copy-start.13
  541.8 3.4 copy-start.14
Sparse Core Ops, SparseCore 0:
  10.2 40.7 all-gather.12
  53.1 35.5 all-gather.14
  90.9 35.5 all-gather.16
  128.6 35.5 all-gather.20
  166.2 35.5 all-gather.22
  203.8 35.5 all-gather.18
  286.1 37.0 reduce-scatter.14
  325.6 37.2 reduce-scatter.16
  365.3 37.2 reduce-scatter.10
  404.8 37.1 reduce-scatter.12
  444.4 37.1 reduce-scatter.6
  483.9 37.1 reduce-scatter.8
where the time goes:
time: 564 us; the launch traced here: 555 us
  waiting for transfers between devices  329 us (58%)
  matrix products  160 us (28%)
  between operations  17.6 us (3%)
  local copies, waits for them, and re-layouts  17.3 us (3%)
  blocking collectives  16.1 us (3%)
  other arithmetic  14.4 us (3%)
    all_gather x6, waiting for transfers between devices, fetched(): lax.all_gather(w[number], 'dp', axis=0, tiled=True)  164 us
    reduce_scatter x6, waiting for transfers between devices, step(): lax.psum_scatter(by_w[name], 'dp', scatter_dimension=0, tiled=True)  163 us
    dot_general x5, matrix products, layer(): gate = jnp.dot(a, w['w_gate'], preferred_element_type=jnp.float32)  60.6 us
    dot_general x5, matrix products, layer(): up = jnp.dot(a, w['w_up'], preferred_element_type=jnp.float32)  51.4 us
    dot_general x5, matrix products, matmul(): jnp.dot(a, w, preferred_element_type=jnp.float32).astype(jnp.bfloat16)  47.8 us
    psum x1, blocking collectives, step(): squares = lax.psum(sum((jnp.sum(g * g) for g in gradients)), 'dp')  16.1 us
    unnamed x44, local copies, waits for them, and re-layouts  11.6 us
  transfers between devices with their start and end apart: 12, of which 11 were waited for; matrix products, arithmetic and copies ran while one was open for 24% of the time, Pallas kernels for 0%

commit v1 on v0

v1 whole, which is shorter than its diff:
```python
import functools

import jax
import jax.numpy as jnp
from jax import lax
from jax.experimental import pallas as pl
from jax.experimental.pallas import tpu as pltpu
from jax.sharding import PartitionSpec as P

BF, F32 = jnp.bfloat16, jnp.float32
TILE = 512
CH = 512


def mm(a, b):
    return jnp.dot(a, b, preferred_element_type=F32)


def mm_nt(a, b):
    return lax.dot_general(a, b, (((1,), (1,)), ((), ())), preferred_element_type=F32)


def scale_of(wide):
    return lax.rsqrt(jnp.mean(wide * wide, -1, keepdims=True) + 1e-6)


def kernel(n, x_hbm, dy_hbm, wg_in, wu_in, wd_in, og, ou, od, oss, *scratch):
    (wg, wu, wd, rg, ru, rd, mid, dg, du, at, dt, xb, yb, mine, theirs,
     aga_s, aga_r, agb_s, agb_r, agp_s, agp_r, rsa_s, rsa_r, rsb_s, rsb_r, all_s, all_r, loc) = scratch
    rep, z = lax.axis_index("rep"), lax.axis_index("dp")
    core = lax.rem(rep, 2)
    way = 1 - 2 * core
    ha = n // 2
    hb = n - 1 - ha
    tokens, d = xb.shape
    ff = mid.shape[1]

    def at_z(k):
        return lax.rem(z + way * k + n, n)

    near, far = at_z(1), at_z(-1)
    near_id, far_id, pair_id = (rep, near), (rep, far), (rep + way, z)

    barrier = pltpu.get_barrier_semaphore()
    for k in range(1, n):
        pl.semaphore_signal(barrier, inc=1, device_id=(rep, lax.rem(z + k, n)), device_id_type=pl.DeviceIdType.MESH)
    pl.semaphore_signal(barrier, inc=1, device_id=pair_id, device_id_type=pl.DeviceIdType.MESH)
    pl.semaphore_wait(barrier, n)

    full, shard, got, out = (wg, wu, wd), (wg_in, wu_in, wd_in), (rg, ru, rd), (og, ou, od)

    def half_of(i, ref, slot, block):
        rows, cols = shard[i].shape[1:]
        if i == 2:
            return ref.at[slot, pl.ds(pl.multiple_of(block * rows + core * (rows // 2), 16), rows // 2), :]
        return ref.at[slot, pl.ds(pl.multiple_of(block * rows, 16), rows), pl.ds(pl.multiple_of(core * (cols // 2), 128), cols // 2)]

    def rows_of(i, ref, slot, block):
        rows = shard[i].shape[1]
        return ref.at[slot, pl.ds(pl.multiple_of(block * rows, 16), rows), :]

    def remote(src, dst, send, recv, to):
        return pltpu.make_async_remote_copy(
            src_ref=src, dst_ref=dst, send_sem=send, recv_sem=recv, device_id=to, device_id_type=pl.DeviceIdType.MESH
        )

    def ag_a(m, s):
        i, l = m % 3, m // 3
        dst = half_of(i, full[i], l, at_z(-s))
        src = half_of(i, shard[i], l, 0) if s == 0 else dst
        return remote(src, dst, aga_s.at[m, s], aga_r.at[m, s], near_id)

    def ag_b(m, s):
        i, l = m % 3, m // 3
        dst = half_of(i, full[i], l, at_z(s))
        src = half_of(i, shard[i], l, 0) if s == 0 else dst
        return remote(src, dst, agb_s.at[m, s], agb_r.at[m, s], far_id)

    def ag_p(m, k):
        i, l = m % 3, m // 3
        block = at_z(-(k + 1)) if k < ha else at_z(k - ha + 1)
        ref = half_of(i, full[i], l, block)
        return remote(ref, ref, agp_s.at[m, k], agp_r.at[m, k], pair_id)

    def ag_tick(m, s):
        if s == 0:
            ag_a(m, 0).start()
            ag_b(m, 0).start()
            i, l = m % 3, m // 3
            rows = shard[i].shape[1]
            full[i][l, pl.ds(pl.multiple_of(z * rows, 16), rows), :] = shard[i][l]
            return
        if s <= ha:
            ag_a(m, s - 1).wait_recv()
            if s < ha:
                ag_a(m, s).start()
            ag_p(m, s - 1).start()
        if s <= hb:
            ag_b(m, s - 1).wait_recv()
            if s < hb:
                ag_b(m, s).start()
            ag_p(m, ha + s - 1).start()

    def ag_done(m):
        for k in range(n - 1):
            ag_p(m, k).wait_recv()

    def ag_drain(m):
        for s in range(ha):
            ag_a(m, s).wait_send()
        for s in range(hb):
            ag_b(m, s).wait_send()
        for k in range(n - 1):
            ag_p(m, k).wait_send()

    def slot_of(m):
        return 2 if m // 3 else 1

    def rs_a(m, s):
        i = m % 3
        src = rows_of(i, full[i], slot_of(m), at_z(ha - s))
        return remote(src, got[i].at[m // 3, s], rsa_s.at[m, s], rsa_r.at[m, s], near_id)

    def rs_b(m, s):
        i = m % 3
        src = rows_of(i, full[i], slot_of(m), at_z(-(hb - s)))
        return remote(src, got[i].at[m // 3, ha + s], rsb_s.at[m, s], rsb_r.at[m, s], far_id)

    def add_in(m, block, k):
        ref = rows_of(m % 3, full[m % 3], slot_of(m), block)
        ref[...] = (ref[...].astype(F32) + got[m % 3][m // 3, k].astype(F32)).astype(BF)

    def rs_tick(m, s):
        i = m % 3
        if s < ha:
            if s:
                rs_a(m, s - 1).wait_recv()
                add_in(m, at_z(ha - s), s - 1)
            rs_a(m, s).start()
        if 1 <= s <= hb:
            if s > 1:
                rs_b(m, s - 2).wait_recv()
                add_in(m, at_z(-(hb - s + 1)), ha + s - 2)
            rs_b(m, s - 1).start()
        if s == ha:
            rs_a(m, ha - 1).wait_recv()
            rs_b(m, hb - 1).wait_recv()
            own = rows_of(i, full[i], slot_of(m), z)[...].astype(F32)
            g = (own + got[i][m // 3, ha - 1].astype(F32) + got[i][m // 3, n - 2].astype(F32)).astype(BF)
            out[i][m // 3] = g
            wide = g.astype(F32)
            mine[...] += jnp.full(mine.shape, jnp.sum(wide * wide), F32)

    def rs_drain(m):
        for s in range(ha):
            rs_a(m, s).wait_send()
        for s in range(hb):
            rs_b(m, s).wait_send()

    def run(ticks):
        for kind, m, s in ticks:
            (ag_tick if kind == "a" else rs_tick)(m, s)

    def loop(steps, pieces, body, sched):
        def one(t, carry):
            for c in range(pieces):
                body(t, c)
                for (when, piece), ticks in sched.items():
                    if piece == c:
                        pl.when(t == when)(functools.partial(run, ticks))
            return carry

        lax.fori_loop(0, steps, one, 0)

    G0, U0, D0, G1, U1, D1 = range(6)
    steps, pieces = tokens // TILE, ff // CH
    mine[...] = jnp.zeros_like(mine)
    get_x = pltpu.make_async_copy(x_hbm, xb, loc.at[0])
    get_dy = pltpu.make_async_copy(dy_hbm, yb, loc.at[1])
    get_x.start()
    get_dy.start()

    a = lambda m, s: ("a", m, s)
    r = lambda m, s: ("r", m, s)
    run([a(G0, 0), a(U0, 0), a(G0, 1), a(U0, 1), a(G0, 2), a(U0, 2), a(D0, 0), a(G0, 3), a(U0, 3), a(G1, 0), a(G0, 4), a(U0, 4)])
    get_x.wait()
    run([a(D0, 1), a(G1, 1)])
    ag_done(G0)
    ag_done(U0)

    def rows_at(t):
        return pl.ds(pl.multiple_of(t * TILE, TILE), TILE)

    def cols(c):
        return pl.ds(c * CH, CH)

    def first(t, c):
        rows = rows_at(t)
        if c == 0:
            wide = xb[rows, :].astype(F32)
            a_tile = (wide * scale_of(wide)).astype(BF)
            du[rows, pl.ds(0, d)] = a_tile
        a_tile = du[rows, pl.ds(0, d)]
        gate, up = mm(a_tile, wg[0, :, cols(c)]), mm(a_tile, wu[0, :, cols(c)])
        mid[rows, cols(c)] = (gate * jax.nn.sigmoid(gate) * up).astype(BF)

    loop(steps, pieces, first, {
        (0, 1): [a(D0, 2), a(G1, 2)], (1, 0): [a(D0, 3), a(G1, 3), a(U1, 0)], (1, 2): [a(D1, 0), a(D0, 4), a(G1, 4)],
        (2, 2): [a(U1, 1), a(D1, 1)],
    })
    run([a(U1, 2), a(D1, 2)])
    ag_done(D0)

    def down(t, c):
        rows = rows_at(t)
        xb[rows, :] = (xb[rows, :].astype(F32) + mm(mid[rows, :], wd[0]).astype(BF).astype(F32)).astype(BF)

    loop(steps, 1, down, {(1, 0): [a(U1, 3), a(D1, 3)], (3, 0): [a(U1, 4), a(D1, 4)]})
    get_dy.wait()
    for m in (G1, U1, D1):
        ag_done(m)

    def hidden(l, h_ref, ct_ref):
        def body(t, c):
            rows = rows_at(t)
            if c == 0:
                wide = h_ref[rows, :].astype(F32)
                a_tile = (wide * scale_of(wide)).astype(BF)
                du[rows, pl.ds((pieces - 1) * CH, d - CH)] = a_tile[:, CH:]
                dg[rows, pl.ds((pieces - 1) * CH, CH)] = a_tile[:, :CH]
                at[:, rows] = a_tile.T
                dt[:, rows] = ct_ref[rows, :].T
            a_tile = jnp.concatenate(
                [dg[rows, pl.ds((pieces - 1) * CH, CH)], du[rows, pl.ds((pieces - 1) * CH, d - CH)]], axis=1
            )
            gate, up = mm(a_tile, wg[l, :, cols(c)]), mm(a_tile, wu[l, :, cols(c)])
            ct = mm_nt(ct_ref[rows, :], wd[l, cols(c), :]).astype(BF).astype(F32)
            s = jax.nn.sigmoid(gate)
            silu = gate * s
            mid[rows, cols(c)] = (silu * up).astype(BF)
            du[rows, cols(c)] = (ct * silu).astype(BF)
            by_silu = ct * up
            dg[rows, cols(c)] = (by_silu * (s * (1.0 + gate * (1.0 - s)))).astype(BF)

        return body

    loop(steps, pieces, hidden(1, xb, yb), {})
    for m in (G1, U1, D1):
        ag_drain(m)

    DC = ff // 4

    def term_down(slot):
        def body(c, _):
            cut = pl.ds(pl.multiple_of(c * DC, DC), DC)
            wd[slot, cut, :] = mm(dt[...], mid[:, cut]).astype(BF).T

        return body

    def term(ref, slot, by):
        def body(c, _):
            cut = pl.ds(pl.multiple_of(c * CH, CH), CH)
            ref[slot, :, cut] = mm(at[...], by[:, cut]).astype(BF)

        return body

    loop(ff // DC, 1, term_down(2), {})
    run([r(D1, 0)])
    loop(pieces, 1, term(wg, 2, dg), {(1, 0): [r(D1, 1)]})
    run([r(G1, 0)])
    loop(pieces, 1, term(wu, 2, du), {(0, 0): [r(D1, 2)], (1, 0): [r(G1, 1)]})
    run([r(U1, 0)])

    def by_input(t, c):
        rows = rows_at(t)
        wide = xb[rows, :].astype(F32)
        ct = mm_nt(dg[rows, :], wg[1]).astype(BF).astype(F32) + mm_nt(du[rows, :], wu[1]).astype(BF).astype(F32)
        ct = ct.astype(BF).astype(F32)
        scale = scale_of(wide)
        inner = jnp.sum(ct * wide, -1, keepdims=True) * (scale * scale * scale) * (1.0 / d)
        by_h = (ct * scale - wide * inner).astype(BF)
        xb[rows, :] = (yb[rows, :].astype(F32) + by_h.astype(F32)).astype(BF)

    loop(steps, 1, by_input, {(0, 0): [r(D1, 3), r(G1, 2)], (1, 0): [r(U1, 1)], (2, 0): [r(D1, 4), r(G1, 3)], (3, 0): [r(U1, 2)]})
    get_x = pltpu.make_async_copy(x_hbm, yb, loc.at[0])
    get_x.start()
    get_x.wait()

    loop(steps, pieces, hidden(0, yb, xb), {(0, 2): [r(G1, 4), r(U1, 3)], (2, 0): [r(U1, 4)]})
    loop(ff // DC, 1, term_down(1), {})
    run([r(D0, 0)])
    loop(pieces, 1, term(wg, 1, dg), {(1, 0): [r(D0, 1)]})
    run([r(G0, 0)])
    loop(pieces, 1, term(wu, 1, du), {(0, 0): [r(D0, 2)], (1, 0): [r(G0, 1)]})
    run([r(U0, 0)])
    run([r(D0, 3), r(G0, 2), r(U0, 1), r(D0, 4), r(G0, 3), r(U0, 2), r(G0, 4), r(U0, 3), r(U0, 4)])

    def tell(k):
        return remote(mine, theirs.at[z], all_s.at[k - 1], all_r.at[k - 1], (rep, lax.rem(z + k, n)))

    for k in range(1, n):
        tell(k).start()
    theirs[z] = mine[...]
    for m in (G0, U0, D0):
        ag_drain(m)
    for m in range(6):
        rs_drain(m)
    for k in range(1, n):
        tell(k).wait()
    oss[...] = jnp.sum(theirs[...], axis=0)


def adamw(w, m, v, g):
    m = 0.9 * m + 0.1 * g
    v = 0.95 * v + 0.05 * g * g
    step = m * lax.rsqrt(v + 1e-8) + 0.1 * w
    return (w - 0.02 * step).astype(BF), m, v


def clipped(gradients, sum_of_squares, count):
    factor = jnp.minimum(1.0, 0.5 * lax.rsqrt(sum_of_squares / count + 1e-30))
    return [g * factor for g in gradients]


def solution(mesh):
    n = mesh.shape["dp"]

    def step(x, dy, *arrays):
        weights, m, v = (arrays[i : i + 3] for i in (0, 3, 6))
        x, dy = x[0], dy[0]
        tokens, d = x.shape
        ff = weights[0].shape[2]
        ha, hb = n // 2, n - 1 - n // 2
        vmem = pl.BlockSpec(memory_space=pltpu.VMEM)
        anywhere = pl.BlockSpec(memory_space=pl.ANY)
        dma = pltpu.SemaphoreType.DMA
        flops = 17 * 2 * tokens * d * ff
        *gradients, squares = pl.pallas_call(
            functools.partial(kernel, n),
            out_shape=[jax.ShapeDtypeStruct(w.shape, BF) for w in weights] + [jax.ShapeDtypeStruct((8, 128), F32)],
            in_specs=[anywhere, anywhere, vmem, vmem, vmem],
            out_specs=[vmem] * 4,
            scratch_shapes=[
                pltpu.VMEM((3, d, ff), BF),
                pltpu.VMEM((3, d, ff), BF),
                pltpu.VMEM((3, ff, d), BF),
                *[pltpu.VMEM((2, n - 1, *w.shape[1:]), BF) for w in weights],
                *[pltpu.VMEM((tokens, ff), BF)] * 3,
                *[pltpu.VMEM((d, tokens), BF)] * 2,
                *[pltpu.VMEM((tokens, d), BF)] * 2,
                pltpu.VMEM((8, 128), F32),
                pltpu.VMEM((n, 8, 128), F32),
                dma((6, ha)), dma((6, ha)), dma((6, hb)), dma((6, hb)), dma((6, n - 1)), dma((6, n - 1)),
                dma((6, ha)), dma((6, ha)), dma((6, hb)), dma((6, hb)), dma((n - 1,)), dma((n - 1,)), dma((2,)),
            ],
            compiler_params=pltpu.CompilerParams(collective_id=0, has_side_effects=True, vmem_limit_bytes=67043328),
            cost_estimate=pl.CostEstimate(flops=flops, bytes_accessed=10 * tokens * d, transcendentals=0),
        )(x, dy, *weights)
        gradients = [g.astype(F32) for g in gradients]
        gradients = clipped(gradients, squares[0, 0], n * sum(g.size for g in gradients))
        new = [adamw(w.astype(F32), m, v, g) for w, m, v, g in zip(weights, m, v, gradients, strict=True)]
        return tuple(one[which] for which in range(3) for one in new)

    states, cut = P(("rep", "dp"), None, None), P(None, "dp", None)
    return jax.shard_map(
        step,
        mesh=mesh,
        in_specs=(states, states) + (cut,) * 9,
        out_specs=(P("rep", "dp", None),) * 9,
        check_vma=False,
    )
```

time: 564 us -> 255 us (0.45); the launches traced: 555 us -> 255 us
  waiting for transfers between devices: 329 us -> 0 us
  Pallas kernels: 0 us -> 245 us
  matrix products: 160 us -> 0 us
  between operations: 17.6 us -> 1.4 us
  blocking collectives: 16.1 us -> 0 us
  local copies, waits for them, and re-layouts: 17.3 us -> 1.22 us
  other arithmetic: 14.4 us -> 7.35 us
    pallas_call x0 -> x1, Pallas kernels: none -> 245 us  [step(): pl.pallas_call(functools.partial(kernel, n), out_shape=[jax.ShapeDtypeStr...]
    all_gather x6 -> x0, waiting for transfers between devices: 164 us -> none  [fetched(): lax.all_gather(w[number], 'dp', axis=0, tiled=True)]
    reduce_scatter x6 -> x0, waiting for transfers between devices: 163 us -> none  [step(): lax.psum_scatter(by_w[name], 'dp', scatter_dimension=0, tiled=True)]
    dot_general x15 -> x0, matrix products: 160 us -> none  [the longest x5 60.6 us: layer(): gate = jnp.dot(a, w['w_gate'], preferred_element_type=jnp.float32)]
    psum x1 -> x0, blocking collectives: 16.1 us -> none  [step(): squares = lax.psum(sum((jnp.sum(g * g) for g in gradients)), 'dp')]
    unnamed x44 -> x8, local copies, waits for them, and re-layouts: 11.6 us -> 0.02 us
    reduce_sum x4 -> x0, other arithmetic: 6.4 us -> none  [the longest x3 5.84 us: step(): squares = lax.psum(sum((jnp.sum(g * g) for g in gradients)), 'dp')]
  transfers between devices with their start and end apart: 12 -> 0, of which waited for: 11 -> 0; matrix products, arithmetic and copies ran while one was open for 24% -> 0% of each run, Pallas kernels for 0% -> 0%
where the time goes in v1:
time: 255 us
  Pallas kernels  245 us (96%)
  other arithmetic  7.35 us (3%)
    pallas_call x1, Pallas kernels, step(): pl.pallas_call(functools.partial(kernel, n), out_shape=[jax.ShapeDtypeStr...  245 us
    convert_element_type x2, other arithmetic, adamw(): return ((w - 0.02 * step).astype(BF), m, v)  7.35 us

profile of v1, /device:TPU:22, one launch (start us, length us, event | category | flops | bytes accessed | tf_op | source)
XLA Modules:
  0.0 255.0 jit_solution(16014710852448291242)
XLA Ops:
  0.6 245.1 %shard_map.178 = (bf16[2,80,1536]{2,1,0:T(8,128)(2,1)}, bf16[2,80,1536]{2,1,0:T(8,128)(2,1)}, bf16[2,192,640]{2,1,0:T(8,128)(2,1)}, f32[8,128]{1,0:T(8,128)}) custom-call(bf16[2048,640]{1,0:T(8,128)(2,1)} %bitcast.3, bf16[2048,640]{1,0:T(8,128)(2,1)} %bitcast.4, bf16[2,80,1536]{2,1,0:T(8,128)(2,1)} %wg_in.1, bf16[2,80,1536]{2,1,0:T(8,128)(2,1)} %wu_in.1, ...), custom_call_target="tpu_custom_call" | custom-call | flops 68451041280 | bytes 13107200 | tf_op jit(solution)/shard_map/pallas_call | solution.py:338
  245.7 1.2 slice.3
  247.6 0.0 copy-start
  247.6 0.0 copy-start.1
  247.6 0.0 copy-start.2
  247.6 0.0 copy-start.3
  247.6 5.6 %fusion.2 = (bf16[2,80,1536]{2,1,0:T(8,128)(2,1)}, f32[2,80,1536]{2,1,0:T(8,128)}, f32[2,80,1536]{2,1,0:T(8,128)}, bf16[2,80,1536]{2,1,0:T(8,128)(2,1)}, f32[2,80,1536]{2,1,0:T(8,128)}, /*index=5*/f32[2,80,1536]{2,1,0:T(8,128)}) fusion(bf16[2,80,1536]{2,1,0:T(8,128)(2,1)} %wg_in.1, f32[]{:T(128)} %bitcast.2, bf16[2,80,1536]{2,1,0:T(8,128)(2,1)} %get-tuple-element.13, ...), kind=kLoop, calls=%fused_computation.11 | loop fusion | flops 8355840 | bytes 10813444 | tf_op jit(solution)/shard_map/convert_element_type | solution.py:317
  253.3 0.0 copy-done
  253.3 0.0 copy-done.1
  253.3 0.0 copy-done.2
  253.3 0.0 copy-done.3
  253.3 1.7 fusion.8
Async XLA Ops:
  247.6 5.7 %copy-start = (f32[2,192,640]{2,1,0:T(8,128)S(1)}, f32[2,192,640]{2,1,0:T(8,128)}, u32[]{:S(2)}) copy-start(f32[2,192,640]{2,1,0:T(8,128)} %param.21) | copy-start | bytes 2949124
  247.6 5.7 %copy-start.1 = (f32[2,192,640]{2,1,0:T(8,128)S(1)}, f32[2,192,640]{2,1,0:T(8,128)}, u32[]{:S(2)}) copy-start(f32[2,192,640]{2,1,0:T(8,128)} %param.18) | copy-start | bytes 2949124
  247.6 5.7 %copy-start.2 = (bf16[2,192,640]{2,1,0:T(8,128)(2,1)S(1)}, bf16[2,192,640]{2,1,0:T(8,128)(2,1)}, u32[]{:S(2)}) copy-start(bf16[2,192,640]{2,1,0:T(8,128)(2,1)} %wd_in.1) | copy-start | bytes 1474564
  247.6 5.7 %copy-start.3 = (bf16[2,192,640]{2,1,0:T(8,128)(2,1)S(1)}, bf16[2,192,640]{2,1,0:T(8,128)(2,1)}, u32[]{:S(2)}) copy-start(bf16[2,192,640]{2,1,0:T(8,128)(2,1)} %get-tuple-element.16) | copy-start | bytes 1474564

commit v2 on v1

v2 whole, which is shorter than its diff:
```python
import functools

import jax
import jax.numpy as jnp
from jax import lax
from jax.experimental import pallas as pl
from jax.experimental.pallas import tpu as pltpu
from jax.sharding import PartitionSpec as P

BF, F32 = jnp.bfloat16, jnp.float32
TILE = 512
CH = 512
LAG = 1.8


def mm(a, b):
    return jnp.dot(a, b, preferred_element_type=F32)


def mm_nt(a, b):
    return lax.dot_general(a, b, (((1,), (1,)), ((), ())), preferred_element_type=F32)


def scale_of(wide):
    return lax.rsqrt(jnp.mean(wide * wide, -1, keepdims=True) + 1e-6)


def plan(segments, hops, pieces):
    now, free, todo, agenda = 0.0, 0.0, [], {}

    def start(tick):
        nonlocal free
        l, p, s, _ = tick
        cost = (5.27 if p == 2 * pieces else 1.76) * (0.0 if s == hops else 0.5 if s == hops - 1 else 1.0)
        free = max(free, now) + cost
        tick[2:] = [s + 1, free + LAG]
        return (l, p, s)

    for l, kind, steps, each in segments:
        for step in range(steps):
            now += each
            if kind[:4] == "term":
                todo.append([l, step * pieces + int(kind[4:]), 0, now])
            if kind == "down" and step == steps - 1:
                todo.append([l, 2 * pieces, 0, now])
            due = sorted((t for t in todo if t[3] <= now), key=lambda t: t[3])
            if due:
                agenda[l, kind, step] = [start(t) for t in due]
            todo = [t for t in todo if t[2] <= hops]
    after = []
    while todo:
        tick = min(todo, key=lambda t: t[3])
        now = max(now, tick[3])
        after.append(start(tick))
        todo = [t for t in todo if t[2] <= hops]
    return agenda | {"after": after}


def kernel(n, x_hbm, dy_hbm, wg_in, wu_in, wd_in, og, ou, od, oss, *scratch):
    (wg, wu, wd, rg, ru, rd, mid, dg, du, at, dt, xb, yb, mine, theirs,
     agz_s, agz_r, agy_s, agy_r, agp_s, agp_r, rsa_s, rsa_r, rsb_s, rsb_r, all_s, all_r, loc) = scratch
    rep, z = lax.axis_index("rep"), lax.axis_index("dp")
    core = lax.rem(rep, 2)
    way = 1 - 2 * core
    chip = lax.rem(rep // 2, 2)
    ha = n // 2
    hb = n - 1 - ha
    tokens, d = xb.shape
    ff = mid.shape[1]

    def at_z(k):
        return lax.rem(z + way * k + n, n)

    near, far = at_z(1), at_z(-1)
    near_id, far_id, pair_id, side_id = (rep, near), (rep, far), (rep + way, z), (rep + 2 - 4 * chip, z)

    barrier = pltpu.get_barrier_semaphore()
    for k in range(1, n):
        pl.semaphore_signal(barrier, inc=1, device_id=(rep, lax.rem(z + k, n)), device_id_type=pl.DeviceIdType.MESH)
    for other in (pair_id, side_id):
        pl.semaphore_signal(barrier, inc=1, device_id=other, device_id_type=pl.DeviceIdType.MESH)
    with jax.named_scope("entry"):
        pl.semaphore_wait(barrier, n + 1)

    steps, pieces = tokens // TILE, ff // CH
    full, shard, got, out = (wg, wu, wd), (wg_in, wu_in, wd_in), (rg, ru, rd), (og, ou, od)

    def cut_of(i, ref, slot, block, first, count):
        rows, cols = shard[i].shape[1:]
        if i == 2:
            third = rows // 6
            return ref.at[slot, pl.ds(pl.multiple_of(block * rows + core * (3 * third) + first * third, 16), count * third), :]
        third = cols // 6
        return ref.at[
            slot, pl.ds(pl.multiple_of(block * rows, 16), rows), pl.ds(pl.multiple_of(core * (3 * third) + first * third, 128), count * third)
        ]

    def remote(src, dst, send, recv, to):
        return pltpu.make_async_remote_copy(
            src_ref=src, dst_ref=dst, send_sem=send, recv_sem=recv, device_id=to, device_id_type=pl.DeviceIdType.MESH
        )

    def block_of(hop):
        return at_z(-(hop + 1)) if hop < ha else at_z(hop - ha + 1)

    def ag_ring(m, hop):
        i, l = m % 3, m // 3
        s = hop if hop < ha else hop - ha
        block = at_z(-s) if hop < ha else at_z(s)
        dst = cut_of(i, full[i], l, block, chip, 2)
        src = cut_of(i, shard[i], l, 0, chip, 2) if s == 0 else dst
        return remote(src, dst, agz_s.at[m, hop], agz_r.at[m, hop], near_id if hop < ha else far_id)

    def ag_side(m, hop):
        ref = cut_of(m % 3, full[m % 3], m // 3, block_of(hop), 2 * chip, 1)
        return remote(ref, ref, agy_s.at[m, hop], agy_r.at[m, hop], side_id)

    def ag_pair(m, hop, from_side):
        first, count = (2 - 2 * chip, 1) if from_side else (chip, 2)
        ref = cut_of(m % 3, full[m % 3], m // 3, block_of(hop), first, count)
        k = from_side * (n - 1) + hop
        return remote(ref, ref, agp_s.at[m, k], agp_r.at[m, k], pair_id)

    def ag_tick(m, s):
        if s == 0:
            ag_ring(m, 0).start()
            ag_ring(m, ha).start()
            i, l = m % 3, m // 3
            rows = shard[i].shape[1]
            full[i][l, pl.ds(pl.multiple_of(z * rows, 16), rows), :] = shard[i][l]
        for base, hops in ((0, ha), (ha, hb)):
            if 1 <= s <= hops:
                hop = base + s - 1
                ag_ring(m, hop).wait_recv()
                if s < hops:
                    ag_ring(m, hop + 1).start()
                ag_side(m, hop).start()
                ag_pair(m, hop, False).start()
        for base, hops in ((0, ha), (ha, hb)):
            if 2 <= s <= hops + 1:
                hop = base + s - 2
                ag_side(m, hop).wait_recv()
                ag_pair(m, hop, True).start()

    def ag_done(m):
        with jax.named_scope(f"done{m}"):
            for hop in range(n - 1):
                ag_pair(m, hop, False).wait_recv()
                ag_pair(m, hop, True).wait_recv()

    def ag_drain(m):
        for hop in range(n - 1):
            ag_ring(m, hop).wait_send()
            ag_side(m, hop).wait_send()
            ag_pair(m, hop, False).wait_send()
            ag_pair(m, hop, True).wait_send()

    def parts_of(l, p):
        i = p // pieces
        return i, pl.ds(p % pieces * CH, CH) if i < 2 else slice(None), l * (2 * pieces + 1) + p

    def rs_ref(i, l, block, cut):
        rows = shard[i].shape[1]
        return full[i].at[1 + l, pl.ds(pl.multiple_of(block * rows, 16), rows), cut]

    def rs_a(l, p, s):
        i, cut, sem = parts_of(l, p)
        return remote(rs_ref(i, l, at_z(ha - s), cut), got[i].at[l, s, :, cut], rsa_s.at[sem, s], rsa_r.at[sem, s], near_id)

    def rs_b(l, p, s):
        i, cut, sem = parts_of(l, p)
        return remote(rs_ref(i, l, at_z(-(hb - s)), cut), got[i].at[l, ha + s, :, cut], rsb_s.at[sem, s], rsb_r.at[sem, s], far_id)

    def rs_tick(l, p, s):
        i, cut, _ = parts_of(l, p)
        for copy, hops, base, sense in ((rs_a, ha, 0, 1), (rs_b, hb, ha, -1)):
            if s and s <= hops:
                copy(l, p, s - 1).wait_recv()
            if s < hops:
                if s:
                    ref = rs_ref(i, l, at_z(sense * (hops - s)), cut)
                    ref[...] = (ref[...].astype(F32) + got[i][l, base + s - 1, :, cut].astype(F32)).astype(BF)
                copy(l, p, s).start()
        if s == ha:
            own = rs_ref(i, l, z, cut)[...].astype(F32)
            g = (own + got[i][l, ha - 1, :, cut].astype(F32) + got[i][l, n - 2, :, cut].astype(F32)).astype(BF)
            out[i][l, :, cut] = g
            wide = g.astype(F32)
            mine[...] += jnp.full(mine.shape, jnp.sum(wide * wide), F32)

    def rs_drain(l, p):
        for s in range(ha):
            rs_a(l, p, s).wait_send()
        for s in range(hb):
            rs_b(l, p, s).wait_send()

    def run(ticks):
        for m, *s in ticks:
            with jax.named_scope(f"t{m}{s}"):
                rs_tick(m, *s) if len(s) == 2 else ag_tick(m, *s)

    def loop(steps, pieces, body, sched, name="loop"):
        def one(t, carry):
            for c in range(pieces):
                body(t, c)
                for (when, piece), ticks in sched.items():
                    if piece == c:
                        pl.when(t == when)(functools.partial(run, ticks))
            return carry

        with jax.named_scope(name):
            lax.fori_loop(0, steps, one, 0)

    G0, U0, D0, G1, U1, D1 = range(6)
    mine[...] = jnp.zeros_like(mine)
    get_x = pltpu.make_async_copy(x_hbm, xb, loc.at[0])
    get_dy = pltpu.make_async_copy(dy_hbm, yb, loc.at[1])
    get_x.start()
    get_dy.start()

    a = lambda m, s: (m, s)
    run([a(m, s) for s in range(ha) for m in (G0, U0, D0)])
    run([a(G1, 0), a(G0, 4), a(U1, 0), a(U0, 4), a(D1, 0), a(D0, 4), a(G0, 5), a(U0, 5), a(G1, 1), a(D0, 5)])
    get_x.wait()
    for m in (G0, U0, D0):
        ag_done(m)

    def rows_at(t):
        return pl.ds(pl.multiple_of(t * TILE, TILE), TILE)

    def cols(c):
        return pl.ds(c * CH, CH)

    def first(t, c):
        rows = rows_at(t)
        if c == 0:
            wide = xb[rows, :].astype(F32)
            a_tile = (wide * scale_of(wide)).astype(BF)
            du[rows, pl.ds(0, d)] = a_tile
        a_tile = du[rows, pl.ds(0, d)]
        gate, up = mm(a_tile, wg[0, :, cols(c)]), mm(a_tile, wu[0, :, cols(c)])
        mid[rows, cols(c)] = (gate * jax.nn.sigmoid(gate) * up).astype(BF)

    loop(steps, pieces, first, {
        (0, 0): [a(U1, 1)], (0, 2): [a(D1, 1)], (1, 0): [a(G1, 2)], (1, 2): [a(U1, 2)], (2, 0): [a(D1, 2)], (2, 2): [a(G1, 3)],
        (3, 0): [a(U1, 3)], (3, 2): [a(D1, 3)],
    }, "first")

    def down(t, c):
        rows = rows_at(t)
        xb[rows, :] = (xb[rows, :].astype(F32) + mm(mid[rows, :], wd[0]).astype(BF).astype(F32)).astype(BF)

    loop(steps, 1, down, {(0, 0): [a(G1, 4)], (1, 0): [a(U1, 4)], (2, 0): [a(D1, 4), a(G1, 5)], (3, 0): [a(U1, 5), a(D1, 5)]}, "down0")
    get_dy.wait()
    for m in (G1, U1, D1):
        ag_done(m)

    DC = ff // 4
    segments = []
    for l in (1, 0):
        segments += [(l, "prep", steps, 0.6)]
        for p in range(pieces):
            segments += [(l, f"hidden{p}", steps, 1.6), (l, f"term{p}", 2, 1.5)]
        segments += [(l, "down", ff // DC, 1.6)]
        if l:
            segments += [(l, "input", steps, 3.1)]
    agenda = plan(segments, ha, pieces)

    def hidden(l, h_ref, ct_ref):
        last = (pieces - 1) * CH

        def prep(t, _):
            rows = rows_at(t)
            wide = h_ref[rows, :].astype(F32)
            a_tile = (wide * scale_of(wide)).astype(BF)
            dg[rows, pl.ds(last, CH)] = a_tile[:, :CH]
            du[rows, pl.ds(last, d - CH)] = a_tile[:, CH:]
            at[:, rows] = a_tile.T
            dt[:, rows] = ct_ref[rows, :].T

        def piece(t, cut):
            rows = rows_at(t)
            a_tile = jnp.concatenate([dg[rows, pl.ds(last, CH)], du[rows, pl.ds(last, d - CH)]], axis=1)
            gate, up = mm(a_tile, wg[l, :, cut]), mm(a_tile, wu[l, :, cut])
            ct = mm_nt(ct_ref[rows, :], wd[l, cut, :]).astype(BF).astype(F32)
            s = jax.nn.sigmoid(gate)
            silu = gate * s
            mid[rows, cut] = (silu * up).astype(BF)
            du[rows, cut] = (ct * silu).astype(BF)
            dg[rows, cut] = (ct * up * (s * (1.0 + gate * (1.0 - s)))).astype(BF)

        loop(steps, 1, prep, {(t, 0): agenda[l, "prep", t] for t in range(steps) if (l, "prep", t) in agenda}, "prep")

        def one_piece(p, carry):
            cut = pl.ds(pl.multiple_of(p * CH, CH), CH)

            def tile(t, carry):
                piece(t, cut)
                for q in range(pieces):
                    for when in range(steps):
                        if (l, f"hidden{q}", when) in agenda:
                            pl.when((p == q) & (t == when))(functools.partial(run, agenda[l, f"hidden{q}", when]))
                return carry

            with jax.named_scope("hidden"):
                lax.fori_loop(0, steps, tile, 0)
            with jax.named_scope("term"):
                for which, (ref, by) in enumerate(((wg, dg), (wu, du))):
                    ref[1 + l, :, cut] = mm(at[...], by[:, cut]).astype(BF)
                    for q in range(pieces):
                        if (l, f"term{q}", which) in agenda:
                            pl.when(p == q)(functools.partial(run, agenda[l, f"term{q}", which]))
            return carry

        lax.fori_loop(0, pieces, one_piece, 0)

        def term_down(c, _):
            cut = pl.ds(pl.multiple_of(c * DC, DC), DC)
            wd[1 + l, cut, :] = mm(dt[...], mid[:, cut]).astype(BF).T

        loop(ff // DC, 1, term_down, {(t, 0): agenda[l, "down", t] for t in range(ff // DC) if (l, "down", t) in agenda}, "down")

    hidden(1, xb, yb)

    def by_input(t, c):
        rows = rows_at(t)
        wide = xb[rows, :].astype(F32)
        ct = mm_nt(dg[rows, :], wg[1]).astype(BF).astype(F32) + mm_nt(du[rows, :], wu[1]).astype(BF).astype(F32)
        ct = ct.astype(BF).astype(F32)
        scale = scale_of(wide)
        inner = jnp.sum(ct * wide, -1, keepdims=True) * (scale * scale * scale) * (1.0 / d)
        by_h = (ct * scale - wide * inner).astype(BF)
        xb[rows, :] = (yb[rows, :].astype(F32) + by_h.astype(F32)).astype(BF)

    loop(steps, 1, by_input, {(t, 0): agenda[1, "input", t] for t in range(steps) if (1, "input", t) in agenda}, "input")
    get_x = pltpu.make_async_copy(x_hbm, yb, loc.at[0])
    get_x.start()
    for m in (G1, U1, D1):
        ag_drain(m)
    get_x.wait()
    hidden(0, yb, xb)
    run(agenda["after"])

    def tell(k):
        return remote(mine, theirs.at[z], all_s.at[k - 1], all_r.at[k - 1], (rep, lax.rem(z + k, n)))

    for k in range(1, n):
        tell(k).start()
    theirs[z] = mine[...]
    with jax.named_scope("drain"):
      for m in (G0, U0, D0):
        ag_drain(m)
      for l in (0, 1):
          for p in range(2 * pieces + 1):
            rs_drain(l, p)
    with jax.named_scope("tell"):
        for k in range(1, n):
            tell(k).wait()
    oss[...] = jnp.sum(theirs[...], axis=0)


def adamw(w, m, v, g):
    m = 0.9 * m + 0.1 * g
    v = 0.95 * v + 0.05 * g * g
    step = m * lax.rsqrt(v + 1e-8) + 0.1 * w
    return (w - 0.02 * step).astype(BF), m, v


def clipped(gradients, sum_of_squares, count):
    factor = jnp.minimum(1.0, 0.5 * lax.rsqrt(sum_of_squares / count + 1e-30))
    return [g * factor for g in gradients]


def solution(mesh):
    n = mesh.shape["dp"]

    def step(x, dy, *arrays):
        weights, m, v = (arrays[i : i + 3] for i in (0, 3, 6))
        x, dy = x[0], dy[0]
        tokens, d = x.shape
        ff = weights[0].shape[2]
        ha, hb = n // 2, n - 1 - n // 2
        vmem = pl.BlockSpec(memory_space=pltpu.VMEM)
        anywhere = pl.BlockSpec(memory_space=pl.ANY)
        dma = pltpu.SemaphoreType.DMA
        flops = 17 * 2 * tokens * d * ff
        *gradients, squares = pl.pallas_call(
            functools.partial(kernel, n),
            out_shape=[jax.ShapeDtypeStruct(w.shape, BF) for w in weights] + [jax.ShapeDtypeStruct((8, 128), F32)],
            in_specs=[anywhere, anywhere, vmem, vmem, vmem],
            out_specs=[vmem] * 4,
            scratch_shapes=[
                pltpu.VMEM((3, d, ff), BF),
                pltpu.VMEM((3, d, ff), BF),
                pltpu.VMEM((3, ff, d), BF),
                *[pltpu.VMEM((2, n - 1, *w.shape[1:]), BF) for w in weights],
                *[pltpu.VMEM((tokens, ff), BF)] * 3,
                *[pltpu.VMEM((d, tokens), BF)] * 2,
                *[pltpu.VMEM((tokens, d), BF)] * 2,
                pltpu.VMEM((8, 128), F32),
                pltpu.VMEM((n, 8, 128), F32),
                dma((6, n - 1)), dma((6, n - 1)), dma((6, n - 1)), dma((6, n - 1)), dma((6, 2 * n - 2)), dma((6, 2 * n - 2)),
                dma((2 * (2 * (ff // CH) + 1), ha)), dma((2 * (2 * (ff // CH) + 1), ha)), dma((2 * (2 * (ff // CH) + 1), hb)), dma((2 * (2 * (ff // CH) + 1), hb)), dma((n - 1,)), dma((n - 1,)), dma((2,)),
            ],
            compiler_params=pltpu.CompilerParams(collective_id=0, has_side_effects=True, vmem_limit_bytes=67043328),
            cost_estimate=pl.CostEstimate(flops=flops, bytes_accessed=10 * tokens * d, transcendentals=0),
        )(x, dy, *weights)
        gradients = [g.astype(F32) for g in gradients]
        gradients = clipped(gradients, squares[0, 0], n * sum(g.size for g in gradients))
        new = [adamw(w.astype(F32), m, v, g) for w, m, v, g in zip(weights, m, v, gradients, strict=True)]
        return tuple(one[which] for which in range(3) for one in new)

    states, cut = P(("rep", "dp"), None, None), P(None, "dp", None)
    return jax.shard_map(
        step,
        mesh=mesh,
        in_specs=(states, states) + (cut,) * 9,
        out_specs=(P("rep", "dp", None),) * 9,
        check_vma=False,
    )
```

time: 255 us -> 212 us (0.83)
  Pallas kernels: 245 us -> 202 us
    pallas_call x1, Pallas kernels: 245 us -> 202 us  [step(): pl.pallas_call(functools.partial(kernel, n), out_shape=[jax.ShapeDtypeStr...]
where the time goes in v2:
time: 212 us
  Pallas kernels  202 us (95%)
  other arithmetic  7.35 us (3%)
    pallas_call x1, Pallas kernels, step(): pl.pallas_call(functools.partial(kernel, n), out_shape=[jax.ShapeDtypeStr...  202 us
    convert_element_type x2, other arithmetic, adamw(): return ((w - 0.02 * step).astype(BF), m, v)  7.35 us

profile of v2, /device:TPU:22, one launch (start us, length us, event | category | flops | bytes accessed | tf_op | source)
XLA Modules:
  0.0 212.1 jit_solution(2302492689022961270)
XLA Ops:
  0.6 202.2 %shard_map.178 = (bf16[2,80,1536]{2,1,0:T(8,128)(2,1)}, bf16[2,80,1536]{2,1,0:T(8,128)(2,1)}, bf16[2,192,640]{2,1,0:T(8,128)(2,1)}, f32[8,128]{1,0:T(8,128)}) custom-call(bf16[2048,640]{1,0:T(8,128)(2,1)} %bitcast.3, bf16[2048,640]{1,0:T(8,128)(2,1)} %bitcast.4, bf16[2,80,1536]{2,1,0:T(8,128)(2,1)} %wg_in.1, bf16[2,80,1536]{2,1,0:T(8,128)(2,1)} %wu_in.1, ...), custom_call_target="tpu_custom_call" | custom-call | flops 68451041280 | bytes 13107200 | tf_op jit(solution)/shard_map/pallas_call | solution.py:387
  202.8 1.2 slice.3
  204.7 0.0 copy-start
  204.7 0.0 copy-start.1
  204.7 0.0 copy-start.2
  204.7 0.0 copy-start.3
  204.7 5.6 %fusion.2 = (bf16[2,80,1536]{2,1,0:T(8,128)(2,1)}, f32[2,80,1536]{2,1,0:T(8,128)}, f32[2,80,1536]{2,1,0:T(8,128)}, bf16[2,80,1536]{2,1,0:T(8,128)(2,1)}, f32[2,80,1536]{2,1,0:T(8,128)}, /*index=5*/f32[2,80,1536]{2,1,0:T(8,128)}) fusion(bf16[2,80,1536]{2,1,0:T(8,128)(2,1)} %wg_in.1, f32[]{:T(128)} %bitcast.2, bf16[2,80,1536]{2,1,0:T(8,128)(2,1)} %get-tuple-element.13, ...), kind=kLoop, calls=%fused_computation.11 | loop fusion | flops 8355840 | bytes 10813444 | tf_op jit(solution)/shard_map/convert_element_type | solution.py:366
  210.4 0.0 copy-done
  210.4 0.0 copy-done.1
  210.4 0.0 copy-done.2
  210.4 0.0 copy-done.3
  210.4 1.7 fusion.8
Async XLA Ops:
  204.7 5.7 %copy-start = (f32[2,192,640]{2,1,0:T(8,128)S(1)}, f32[2,192,640]{2,1,0:T(8,128)}, u32[]{:S(2)}) copy-start(f32[2,192,640]{2,1,0:T(8,128)} %param.21) | copy-start | bytes 2949124
  204.7 5.7 %copy-start.1 = (f32[2,192,640]{2,1,0:T(8,128)S(1)}, f32[2,192,640]{2,1,0:T(8,128)}, u32[]{:S(2)}) copy-start(f32[2,192,640]{2,1,0:T(8,128)} %param.18) | copy-start | bytes 2949124
  204.7 5.7 %copy-start.2 = (bf16[2,192,640]{2,1,0:T(8,128)(2,1)S(1)}, bf16[2,192,640]{2,1,0:T(8,128)(2,1)}, u32[]{:S(2)}) copy-start(bf16[2,192,640]{2,1,0:T(8,128)(2,1)} %wd_in.1) | copy-start | bytes 1474564
  204.7 5.7 %copy-start.3 = (bf16[2,192,640]{2,1,0:T(8,128)(2,1)S(1)}, bf16[2,192,640]{2,1,0:T(8,128)(2,1)}, u32[]{:S(2)}) copy-start(bf16[2,192,640]{2,1,0:T(8,128)(2,1)} %get-tuple-element.16) | copy-start | bytes 1474564

commit v3 on v2

--- a/solution.py
+++ b/solution.py
@@ -10,7 +10,8 @@
 BF, F32 = jnp.bfloat16, jnp.float32
 TILE = 512
 CH = 512
-LAG = 1.8
+LAG = 2
+STEP = 0.2
 
 
 def mm(a, b):
@@ -31,7 +32,7 @@
     def start(tick):
         nonlocal free
         l, p, s, _ = tick
-        cost = (5.27 if p == 2 * pieces else 1.76) * (0.0 if s == hops else 0.5 if s == hops - 1 else 1.0)
+        cost = (2.63 if p >= 2 * pieces else 1.76) * (0.0 if s == hops else 0.5 if s == hops - 1 else 1.0)
         free = max(free, now) + cost
         tick[2:] = [s + 1, free + LAG]
         return (l, p, s)
@@ -42,21 +43,22 @@
             if kind[:4] == "term":
                 todo.append([l, step * pieces + int(kind[4:]), 0, now])
             if kind == "down" and step == steps - 1:
-                todo.append([l, 2 * pieces, 0, now])
-            due = sorted((t for t in todo if t[3] <= now), key=lambda t: t[3])
+                todo += [[l, 2 * pieces, 0, now], [l, 2 * pieces + 1, 0, now]]
+            due = sorted((t for t in todo if t[3] <= now), key=lambda t: (t[2], -t[1]))
             if due:
                 agenda[l, kind, step] = [start(t) for t in due]
             todo = [t for t in todo if t[2] <= hops]
     after = []
     while todo:
-        tick = min(todo, key=lambda t: t[3])
-        now = max(now, tick[3])
+        now = max(now, min(t[3] for t in todo))
+        tick = min((t for t in todo if t[3] <= now), key=lambda t: (t[2], -t[1]))
         after.append(start(tick))
+        now += STEP
         todo = [t for t in todo if t[2] <= hops]
     return agenda | {"after": after}
 
 
-def kernel(n, x_hbm, dy_hbm, wg_in, wu_in, wd_in, og, ou, od, oss, *scratch):
+def kernel(n, x_hbm, dy_hbm, wg_in, wu_in, wd_in, og, ou, od, factor, *scratch):
     (wg, wu, wd, rg, ru, rd, mid, dg, du, at, dt, xb, yb, mine, theirs,
      agz_s, agz_r, agy_s, agy_r, agp_s, agp_r, rsa_s, rsa_r, rsb_s, rsb_r, all_s, all_r, loc) = scratch
     rep, z = lax.axis_index("rep"), lax.axis_index("dp")
@@ -156,35 +158,39 @@
             ag_pair(m, hop, True).wait_send()
 
     def parts_of(l, p):
-        i = p // pieces
-        return i, pl.ds(p % pieces * CH, CH) if i < 2 else slice(None), l * (2 * pieces + 1) + p
-
-    def rs_ref(i, l, block, cut):
-        rows = shard[i].shape[1]
-        return full[i].at[1 + l, pl.ds(pl.multiple_of(block * rows, 16), rows), cut]
+        sem = l * (2 * pieces + 2) + p
+        if p < 2 * pieces:
+            return p // pieces, pl.ds(0, wg_in.shape[1]), pl.ds(p % pieces * CH, CH), sem
+        half = wd_in.shape[1] // 2
+        return 2, pl.ds((p - 2 * pieces) * half, half), slice(None), sem
+
+    def rs_ref(i, l, block, part, cut):
+        return full[i].at[1 + l, pl.ds(pl.multiple_of(block * shard[i].shape[1] + part.start, 16), part.size), cut]
 
     def rs_a(l, p, s):
-        i, cut, sem = parts_of(l, p)
-        return remote(rs_ref(i, l, at_z(ha - s), cut), got[i].at[l, s, :, cut], rsa_s.at[sem, s], rsa_r.at[sem, s], near_id)
+        i, part, cut, sem = parts_of(l, p)
+        return remote(rs_ref(i, l, at_z(ha - s), part, cut), got[i].at[l, s, part, cut], rsa_s.at[sem, s], rsa_r.at[sem, s], near_id)
 
     def rs_b(l, p, s):
-        i, cut, sem = parts_of(l, p)
-        return remote(rs_ref(i, l, at_z(-(hb - s)), cut), got[i].at[l, ha + s, :, cut], rsb_s.at[sem, s], rsb_r.at[sem, s], far_id)
+        i, part, cut, sem = parts_of(l, p)
+        return remote(
+            rs_ref(i, l, at_z(-(hb - s)), part, cut), got[i].at[l, ha + s, part, cut], rsb_s.at[sem, s], rsb_r.at[sem, s], far_id
+        )
 
     def rs_tick(l, p, s):
-        i, cut, _ = parts_of(l, p)
+        i, part, cut, _ = parts_of(l, p)
         for copy, hops, base, sense in ((rs_a, ha, 0, 1), (rs_b, hb, ha, -1)):
             if s and s <= hops:
                 copy(l, p, s - 1).wait_recv()
             if s < hops:
                 if s:
-                    ref = rs_ref(i, l, at_z(sense * (hops - s)), cut)
-                    ref[...] = (ref[...].astype(F32) + got[i][l, base + s - 1, :, cut].astype(F32)).astype(BF)
+                    ref = rs_ref(i, l, at_z(sense * (hops - s)), part, cut)
+                    ref[...] = (ref[...].astype(F32) + got[i][l, base + s - 1, part, cut].astype(F32)).astype(BF)
                 copy(l, p, s).start()
         if s == ha:
-            own = rs_ref(i, l, z, cut)[...].astype(F32)
-            g = (own + got[i][l, ha - 1, :, cut].astype(F32) + got[i][l, n - 2, :, cut].astype(F32)).astype(BF)
-            out[i][l, :, cut] = g
+            own = rs_ref(i, l, z, part, cut)[...].astype(F32)
+            g = (own + got[i][l, ha - 1, part, cut].astype(F32) + got[i][l, n - 2, part, cut].astype(F32)).astype(BF)
+            out[i][l, part, cut] = g
             wide = g.astype(F32)
             mine[...] += jnp.full(mine.shape, jnp.sum(wide * wide), F32)
 
@@ -219,41 +225,49 @@
     get_dy.start()
 
     a = lambda m, s: (m, s)
-    run([a(m, s) for s in range(ha) for m in (G0, U0, D0)])
-    run([a(G1, 0), a(G0, 4), a(U1, 0), a(U0, 4), a(D1, 0), a(D0, 4), a(G0, 5), a(U0, 5), a(G1, 1), a(D0, 5)])
-    get_x.wait()
-    for m in (G0, U0, D0):
-        ag_done(m)
 
     def rows_at(t):
         return pl.ds(pl.multiple_of(t * TILE, TILE), TILE)
 
+    def norm0(t, c):
+        rows = rows_at(t)
+        wide = xb[rows, :].astype(F32)
+        du[rows, pl.ds(0, d)] = (wide * scale_of(wide)).astype(BF)
+
+    def turn(t, c):
+        dt[:, rows_at(t)] = yb[rows_at(t), :].T
+
+    run([a(G0, 0), a(U0, 0)])
+    get_x.wait()
+    loop(steps, 1, norm0, {}, "norm0")
+    run([a(G0, 1), a(U0, 1), a(D0, 0)])
+    get_dy.wait()
+    loop(steps, 1, turn, {}, "turn")
+    run([a(m, s + (m != D0)) for s in range(1, ha - 1) for m in (G0, U0, D0)])
+    run([a(G0, 4), a(G1, 0), a(U0, 4), a(U1, 0), a(D0, 3), a(G0, 5), a(U0, 5), a(D1, 0)])
+    for m in (G0, U0):
+        ag_done(m)
+
     def cols(c):
         return pl.ds(c * CH, CH)
 
     def first(t, c):
         rows = rows_at(t)
-        if c == 0:
-            wide = xb[rows, :].astype(F32)
-            a_tile = (wide * scale_of(wide)).astype(BF)
-            du[rows, pl.ds(0, d)] = a_tile
         a_tile = du[rows, pl.ds(0, d)]
         gate, up = mm(a_tile, wg[0, :, cols(c)]), mm(a_tile, wu[0, :, cols(c)])
         mid[rows, cols(c)] = (gate * jax.nn.sigmoid(gate) * up).astype(BF)
 
     loop(steps, pieces, first, {
-        (0, 0): [a(U1, 1)], (0, 2): [a(D1, 1)], (1, 0): [a(G1, 2)], (1, 2): [a(U1, 2)], (2, 0): [a(D1, 2)], (2, 2): [a(G1, 3)],
-        (3, 0): [a(U1, 3)], (3, 2): [a(D1, 3)],
+        (0, 0): [a(G1, 1)], (0, 1): [a(D0, 4)], (0, 2): [a(U1, 1)], (1, 0): [a(D1, 1), a(D0, 5)], (1, 2): [a(G1, 2)], (2, 0): [a(U1, 2)],
+        (2, 1): [a(D1, 2)], (2, 2): [a(G1, 3)], (3, 0): [a(U1, 3)], (3, 2): [a(D1, 3)],
     }, "first")
+    ag_done(D0)
 
     def down(t, c):
         rows = rows_at(t)
         xb[rows, :] = (xb[rows, :].astype(F32) + mm(mid[rows, :], wd[0]).astype(BF).astype(F32)).astype(BF)
 
-    loop(steps, 1, down, {(0, 0): [a(G1, 4)], (1, 0): [a(U1, 4)], (2, 0): [a(D1, 4), a(G1, 5)], (3, 0): [a(U1, 5), a(D1, 5)]}, "down0")
-    get_dy.wait()
-    for m in (G1, U1, D1):
-        ag_done(m)
+    loop(steps, 1, down, {(0, 0): [a(G1, 4)], (1, 0): [a(U1, 4)], (2, 0): [a(D1, 4)], (3, 0): [a(G1, 5)]}, "down0")
 
     DC = ff // 4
     segments = []
@@ -276,7 +290,8 @@
             dg[rows, pl.ds(last, CH)] = a_tile[:, :CH]
             du[rows, pl.ds(last, d - CH)] = a_tile[:, CH:]
             at[:, rows] = a_tile.T
-            dt[:, rows] = ct_ref[rows, :].T
+            if not l:
+                dt[:, rows] = ct_ref[rows, :].T
 
         def piece(t, cut):
             rows = rows_at(t)
@@ -289,7 +304,11 @@
             du[rows, cut] = (ct * silu).astype(BF)
             dg[rows, cut] = (ct * up * (s * (1.0 + gate * (1.0 - s)))).astype(BF)
 
-        loop(steps, 1, prep, {(t, 0): agenda[l, "prep", t] for t in range(steps) if (l, "prep", t) in agenda}, "prep")
+        ticks = {(t, 0): agenda[l, "prep", t] for t in range(steps) if (l, "prep", t) in agenda}
+        loop(steps, 1, prep, {(1, 0): [a(U1, 5)], (3, 0): [a(D1, 5)]} if l else ticks, "prep")
+        if l:
+            for m in (G1, U1, D1):
+                ag_done(m)
 
         def one_piece(p, carry):
             cut = pl.ds(pl.multiple_of(p * CH, CH), CH)
@@ -351,12 +370,14 @@
       for m in (G0, U0, D0):
         ag_drain(m)
       for l in (0, 1):
-          for p in range(2 * pieces + 1):
+          for p in range(2 * pieces + 2):
             rs_drain(l, p)
     with jax.named_scope("tell"):
         for k in range(1, n):
             tell(k).wait()
-    oss[...] = jnp.sum(theirs[...], axis=0)
+    squares = jnp.sum(theirs[...], axis=0)[:1, :1]
+    count = n * sum(s.size for s in shard)
+    factor[...] = jnp.minimum(1.0, 0.5 * lax.rsqrt(squares / count + 1e-30))
 
 
 def adamw(w, m, v, g):
@@ -364,11 +385,6 @@
     v = 0.95 * v + 0.05 * g * g
     step = m * lax.rsqrt(v + 1e-8) + 0.1 * w
     return (w - 0.02 * step).astype(BF), m, v
-
-
-def clipped(gradients, sum_of_squares, count):
-    factor = jnp.minimum(1.0, 0.5 * lax.rsqrt(sum_of_squares / count + 1e-30))
-    return [g * factor for g in gradients]
 
 
 def solution(mesh):
@@ -384,9 +400,9 @@
         anywhere = pl.BlockSpec(memory_space=pl.ANY)
         dma = pltpu.SemaphoreType.DMA
         flops = 17 * 2 * tokens * d * ff
-        *gradients, squares = pl.pallas_call(
+        *gradients, factor = pl.pallas_call(
             functools.partial(kernel, n),
-            out_shape=[jax.ShapeDtypeStruct(w.shape, BF) for w in weights] + [jax.ShapeDtypeStruct((8, 128), F32)],
+            out_shape=[jax.ShapeDtypeStruct(w.shape, BF) for w in weights] + [jax.ShapeDtypeStruct((1, 1), F32)],
             in_specs=[anywhere, anywhere, vmem, vmem, vmem],
             out_specs=[vmem] * 4,
             scratch_shapes=[
@@ -400,13 +416,12 @@
                 pltpu.VMEM((8, 128), F32),
                 pltpu.VMEM((n, 8, 128), F32),
                 dma((6, n - 1)), dma((6, n - 1)), dma((6, n - 1)), dma((6, n - 1)), dma((6, 2 * n - 2)), dma((6, 2 * n - 2)),
-                dma((2 * (2 * (ff // CH) + 1), ha)), dma((2 * (2 * (ff // CH) + 1), ha)), dma((2 * (2 * (ff // CH) + 1), hb)), dma((2 * (2 * (ff // CH) + 1), hb)), dma((n - 1,)), dma((n - 1,)), dma((2,)),
+                dma((2 * (2 * (ff // CH) + 2), ha)), dma((2 * (2 * (ff // CH) + 2), ha)), dma((2 * (2 * (ff // CH) + 2), hb)), dma((2 * (2 * (ff // CH) + 2), hb)), dma((n - 1,)), dma((n - 1,)), dma((2,)),
             ],
             compiler_params=pltpu.CompilerParams(collective_id=0, has_side_effects=True, vmem_limit_bytes=67043328),
             cost_estimate=pl.CostEstimate(flops=flops, bytes_accessed=10 * tokens * d, transcendentals=0),
         )(x, dy, *weights)
-        gradients = [g.astype(F32) for g in gradients]
-        gradients = clipped(gradients, squares[0, 0], n * sum(g.size for g in gradients))
+        gradients = [g.astype(F32) * factor[0, 0] for g in gradients]
         new = [adamw(w.astype(F32), m, v, g) for w, m, v, g in zip(weights, m, v, gradients, strict=True)]
         return tuple(one[which] for which in range(3) for one in new)
 

time: 212 us -> 207 us (0.976)
  Pallas kernels: 202 us -> 197 us
    pallas_call x1, Pallas kernels: 202 us -> 197 us  [step(): pl.pallas_call(functools.partial(kernel, n), out_shape=[jax.ShapeDtypeStr...]
where the time goes in v3:
time: 207 us
  Pallas kernels  197 us (95%)
  other arithmetic  8.67 us (4%)
    pallas_call x1, Pallas kernels, step(): pl.pallas_call(functools.partial(kernel, n), out_shape=[jax.ShapeDtypeStr...  197 us
    convert_element_type x2, other arithmetic, adamw(): return ((w - 0.02 * step).astype(BF), m, v)  8.67 us

profile of v3, /device:TPU:22, one launch (start us, length us, event | category | flops | bytes accessed | tf_op | source)
XLA Modules:
  0.0 206.6 jit_solution(10984131843540228733)
XLA Ops:
  0.6 197.2 %shard_map.178 = (bf16[2,80,1536]{2,1,0:T(8,128)(2,1)}, bf16[2,80,1536]{2,1,0:T(8,128)(2,1)}, bf16[2,192,640]{2,1,0:T(8,128)(2,1)}, f32[1,1]{1,0:T(1,128)}) custom-call(bf16[2048,640]{1,0:T(8,128)(2,1)} %bitcast.3, bf16[2048,640]{1,0:T(8,128)(2,1)} %bitcast.4, bf16[2,80,1536]{2,1,0:T(8,128)(2,1)} %wg_in.1, bf16[2,80,1536]{2,1,0:T(8,128)(2,1)} %wu_in.1, ...), custom_call_target="tpu_custom_call" | custom-call | flops 68451041280 | bytes 13107200 | tf_op jit(solution)/shard_map/pallas_call | solution.py:403
  197.9 0.0 copy-start
  197.9 0.0 copy-start.1
  197.9 0.0 copy-start.2
  197.9 0.0 copy-start.3
  197.9 6.3 %fusion.2 = (bf16[2,80,1536]{2,1,0:T(8,128)(2,1)}, f32[2,80,1536]{2,1,0:T(8,128)}, f32[2,80,1536]{2,1,0:T(8,128)}, bf16[2,80,1536]{2,1,0:T(8,128)(2,1)}, f32[2,80,1536]{2,1,0:T(8,128)}, /*index=5*/f32[2,80,1536]{2,1,0:T(8,128)}) fusion(bf16[2,80,1536]{2,1,0:T(8,128)(2,1)} %wg_in.1, f32[]{:T(128)} %bitcast.2, bf16[2,80,1536]{2,1,0:T(8,128)(2,1)} %get-tuple-element.13, ...), kind=kLoop, calls=%fused_computation.11 | loop fusion | flops 8355840 | bytes 10813444 | tf_op jit(solution)/shard_map/convert_element_type | solution.py:387
  204.3 0.0 copy-done
  204.3 0.0 copy-done.1
  204.3 0.0 copy-done.2
  204.3 0.0 copy-done.3
  204.3 2.4 %fusion.8 = (bf16[2,192,640]{2,1,0:T(8,128)(2,1)}, f32[2,192,640]{2,1,0:T(8,128)}, f32[2,192,640]{2,1,0:T(8,128)}) fusion(bf16[2,192,640]{2,1,0:T(8,128)(2,1)S(1)} %copy-done.2, f32[]{:T(128)} %bitcast.2, bf16[2,192,640]{2,1,0:T(8,128)(2,1)S(1)} %copy-done.3, f32[2,192,640]{2,1,0:T(8,128)S(1)} %copy-done, f32[2,192,640]{2,1,0:T(8,128)S(1)} %copy-done.1), kind=kLoop, calls=%fused_computation.17 | loop fusion | flops 4177920 | bytes 5406724 | tf_op jit(solution)/shard_map/convert_element_type | solution.py:387
Async XLA Ops:
  197.9 6.4 %copy-start = (f32[2,192,640]{2,1,0:T(8,128)S(1)}, f32[2,192,640]{2,1,0:T(8,128)}, u32[]{:S(2)}) copy-start(f32[2,192,640]{2,1,0:T(8,128)} %param.21) | copy-start | bytes 2949124
  197.9 6.3 %copy-start.1 = (f32[2,192,640]{2,1,0:T(8,128)S(1)}, f32[2,192,640]{2,1,0:T(8,128)}, u32[]{:S(2)}) copy-start(f32[2,192,640]{2,1,0:T(8,128)} %param.18) | copy-start | bytes 2949124
  197.9 6.3 %copy-start.2 = (bf16[2,192,640]{2,1,0:T(8,128)(2,1)S(1)}, bf16[2,192,640]{2,1,0:T(8,128)(2,1)}, u32[]{:S(2)}) copy-start(bf16[2,192,640]{2,1,0:T(8,128)(2,1)} %wd_in.1) | copy-start | bytes 1474564
  197.9 6.3 %copy-start.3 = (bf16[2,192,640]{2,1,0:T(8,128)(2,1)S(1)}, bf16[2,192,640]{2,1,0:T(8,128)(2,1)}, u32[]{:S(2)}) copy-start(bf16[2,192,640]{2,1,0:T(8,128)(2,1)} %get-tuple-element.16) | copy-start | bytes 1474564

commit v4 on v3

--- a/solution.py
+++ b/solution.py
@@ -385,6 +385,12 @@
     v = 0.95 * v + 0.05 * g * g
     step = m * lax.rsqrt(v + 1e-8) + 0.1 * w
     return (w - 0.02 * step).astype(BF), m, v
+
+
+def update(factor, *refs):
+    for i in range(3):
+        w, m, v, g, new_w, new_m, new_v = (refs[3 * k + i] for k in range(7))
+        new_w[...], new_m[...], new_v[...] = adamw(w[...].astype(F32), m[...], v[...], g[...].astype(F32) * factor[...].reshape(1, 1, 1))
 
 
 def solution(mesh):
@@ -421,9 +427,16 @@
             compiler_params=pltpu.CompilerParams(collective_id=0, has_side_effects=True, vmem_limit_bytes=67043328),
             cost_estimate=pl.CostEstimate(flops=flops, bytes_accessed=10 * tokens * d, transcendentals=0),
         )(x, dy, *weights)
-        gradients = [g.astype(F32) * factor[0, 0] for g in gradients]
-        new = [adamw(w.astype(F32), m, v, g) for w, m, v, g in zip(weights, m, v, gradients, strict=True)]
-        return tuple(one[which] for which in range(3) for one in new)
+        blocks = [pl.BlockSpec((1, w.shape[1] // 2, w.shape[2]), lambda l, i: (l, i, 0)) for w in weights]
+        return tuple(
+            pl.pallas_call(
+                update,
+                grid=(weights[0].shape[0], 2),
+                out_shape=[jax.ShapeDtypeStruct(w.shape, dtype) for dtype in (BF, F32, F32) for w in weights],
+                in_specs=[pl.BlockSpec((1, 1), lambda l, i: (0, 0)), *blocks * 4],
+                out_specs=blocks * 3,
+            )(factor, *weights, *m, *v, *gradients)
+        )
 
     states, cut = P(("rep", "dp"), None, None), P(None, "dp", None)
     return jax.shard_map(

time: 207 us -> 206 us (level)
  other arithmetic: 8.67 us -> 0 us
  Pallas kernels: 197 us -> 205 us
    convert_element_type x2 -> x0, other arithmetic: 8.67 us -> none  [adamw(): return ((w - 0.02 * step).astype(BF), m, v)]
    pallas_call x0 -> x1, Pallas kernels: none -> 7.94 us  [step(): pl.pallas_call(update, grid=(weights[0].shape[0], 2), out_shape=[jax.Shap...]
where the time goes in v4:
time: 206 us
  Pallas kernels  205 us (100%)
    pallas_call x1, Pallas kernels, step(): pl.pallas_call(functools.partial(kernel, n), out_shape=[jax.ShapeDtypeStr...  197 us
    pallas_call x1, Pallas kernels, step(): pl.pallas_call(update, grid=(weights[0].shape[0], 2), out_shape=[jax.Shap...  7.94 us

profile of v4, /device:TPU:22, one launch (start us, length us, event | category | flops | bytes accessed | tf_op | source)
XLA Modules:
  0.0 206.0 jit_solution(6593412317871633452)
XLA Ops:
  0.6 197.3 %shard_map.178 = (bf16[2,80,1536]{2,1,0:T(8,128)(2,1)}, bf16[2,80,1536]{2,1,0:T(8,128)(2,1)}, bf16[2,192,640]{2,1,0:T(8,128)(2,1)}, f32[1,1]{1,0:T(1,128)}) custom-call(bf16[2048,640]{1,0:T(8,128)(2,1)} %bitcast.2, bf16[2048,640]{1,0:T(8,128)(2,1)} %bitcast.3, bf16[2,80,1536]{2,1,0:T(8,128)(2,1)} %refs_0_.1, bf16[2,80,1536]{2,1,0:T(8,128)(2,1)} %refs_1_.1, ...), custom_call_target="tpu_custom_call" | custom-call | flops 68451041280 | bytes 13107200 | tf_op jit(solution)/shard_map/pallas_call | solution.py:409
  197.9 7.9 %shard_map.179 = (bf16[2,80,1536]{2,1,0:T(8,128)(2,1)}, bf16[2,80,1536]{2,1,0:T(8,128)(2,1)}, bf16[2,192,640]{2,1,0:T(8,128)(2,1)}, f32[2,80,1536]{2,1,0:T(8,128...) custom-call(f32[1,1]{1,0:T(1,128)} %get-tuple-element.13.factor, ...), custom_call_target="tpu_custom_call" | custom-call | tf_op jit(solution)/shard_map/pallas_call | solution.py:432
